TPU v7x, 32 devices: a 4x4x1 block of a 4x4x8 slice. The times are simulated.
32 devices in a mesh: dp: 1 (over z), cz: 4 (over y), cy: 4 (over x), cx: 2 (over core).
Axes of the slice: x: 4, y: 4, z: 1, core: 2. Of those that a mesh axis runs over, the one named last changes fastest.
The devices are a block of a 4x4x8 slice.
Arguments:
- x_act: bfloat16 [4096, 4096], P(('dp', 'cx', 'cz'), 'cy')
- w_up: bfloat16 [4096, 16384], P('cy', ('cz', 'cx'))
- w_down: bfloat16 [16384, 4096], P('cz', ('cy', 'cx'))
- z_grad: bfloat16 [4096, 4096], P(('dp', 'cx', 'cz'), 'cy')
Outputs:
- output 1: bfloat16 [4096, 4096], P(('dp', 'cx', 'cz'), 'cy')
- output 2: bfloat16 [4096, 16384], P(('dp', 'cy'), ('cz', 'cx'))
- output 3: bfloat16 [16384, 4096], P(('dp', 'cz'), ('cy', 'cx'))
All inputs are finite; a program needn't handle non-finite values.
Results may differ from a plain program's by a relative error of at most 0.0115233.
Values are sent between devices in bfloat16 or wider.
A program may use at most 768 MiB of HBM per device.

v0:
```python
import math
import jax
import jax.numpy as jnp
from jax import lax
from jax.sharding import PartitionSpec as P

GELU_COEF = 0.044715
SQRT_TWO_PI = math.sqrt(2.0 / math.pi)
CONTRACT_LAST = (((1,), (1,)), ((), ()))
CONTRACT_FIRST = (((0,), (0,)), ((), ()))


def gelu_parts(pre_act):
    inner_arg = SQRT_TWO_PI * (pre_act + GELU_COEF * pre_act * pre_act * pre_act)
    tanh_val = jnp.tanh(inner_arg)
    gelu_val = 0.5 * pre_act * (1.0 + tanh_val)
    gelu_slope = 0.5 * (1.0 + tanh_val) + 0.5 * pre_act * (1.0 - tanh_val * tanh_val) * SQRT_TWO_PI * (1.0 + 3.0 * GELU_COEF * pre_act * pre_act)
    return gelu_val, gelu_slope


def solution(mesh):
    row_spec = P(("dp", "cx", "cz"), "cy")
    up_spec = P("cy", ("cz", "cx"))
    down_spec = P("cz", ("cy", "cx"))
    up_out = P(("dp", "cy"), ("cz", "cx"))
    down_out = P(("dp", "cz"), ("cy", "cx"))

    def local_step(x_act, w_up, w_down, z_grad):
        x_full = lax.all_gather(x_act, "cz", axis=0, tiled=True)
        up_full = lax.all_gather(w_up, "cx", axis=1, tiled=True)
        pre_part = jnp.dot(x_full, up_full, preferred_element_type=jnp.float32)
        pre_sum = lax.psum_scatter(pre_part, "cy", scatter_dimension=0, tiled=True)
        pre_act = pre_sum.astype(jnp.bfloat16).astype(jnp.float32)
        gelu_val, gelu_slope = gelu_parts(pre_act)
        hidden = gelu_val.astype(jnp.bfloat16)
        z_full = lax.all_gather(z_grad, "cz", axis=0, tiled=True)
        down_full = lax.all_gather(w_down, "cx", axis=1, tiled=True)
        h_part = lax.dot_general(z_full, down_full, CONTRACT_LAST, preferred_element_type=jnp.float32)
        h_grad = lax.psum_scatter(h_part, "cy", scatter_dimension=0, tiled=True)
        pre_grad = (h_grad * gelu_slope).astype(jnp.bfloat16)
        hidden_full = lax.all_gather(hidden, "cy", axis=0, tiled=True)
        down_part = lax.dot_general(hidden_full, z_full, CONTRACT_FIRST, preferred_element_type=jnp.float32)
        down_grad = lax.psum_scatter(down_part, "cx", scatter_dimension=1, tiled=True).astype(jnp.bfloat16)
        grad_full = lax.all_gather(pre_grad, "cy", axis=0, tiled=True)
        x_part = lax.dot_general(grad_full, up_full, CONTRACT_LAST, preferred_element_type=jnp.float32)
        x_grad = lax.psum_scatter(x_part, "cz", scatter_dimension=0, tiled=True).astype(jnp.bfloat16)
        up_part = lax.dot_general(x_full, grad_full, CONTRACT_FIRST, preferred_element_type=jnp.float32)
        up_grad = lax.psum_scatter(up_part, "cx", scatter_dimension=1, tiled=True).astype(jnp.bfloat16)
        return (x_grad, up_grad, down_grad)

    return jax.shard_map(local_step, mesh=mesh, in_specs=(row_spec, up_spec, down_spec, row_spec), out_specs=(row_spec, up_out, down_out), check_vma=False)
```

profile of v0, /device:TPU:96, one launch (start us, length us, event | category | flops | bytes accessed | tf_op | source)
XLA Modules:
  0.0 1185.6 jit_solution(2225698766435824378)
XLA Ops:
  7.2 0.7 all-gather.7.cloned.1.call-update
  8.0 0.7 all-gather.9.cloned.1.call-update
  10.3 47.4 %all-gather.7.cloned.1.call-done = bf16[2048,1024]{1,0:T(8,128)(2,1)} async-done(((bf16[512,1024]{1,0:T(8,128)(2,1)}), bf16[2048,1024]{1,0:T(8,128)(2,1)}) %all-gather.7.cloned.1.call-update) | async-done | bytes 4194320 | tf_op jit(solution)/shard_map/all_gather | solution.py:36
  57.7 22.7 %all-gather.9.cloned.1.call-done = bf16[4096,1024]{1,0:T(8,128)(2,1)} async-done(((bf16[4096,512]{1,0:T(8,128)(2,1)}), bf16[4096,1024]{1,0:T(8,128)(2,1)}) %all-gather.9.cloned.1.call-update) | async-done | bytes 8388624 | tf_op jit(solution)/shard_map/all_gather | solution.py:37
  80.5 25.2 %fusion.11 = f32[2048,4096]{1,0:T(8,128)} fusion(bf16[2048,1024]{1,0:T(8,128)(2,1)} %all-gather.7.cloned.1.call-done, bf16[4096,1024]{1,0:T(8,128)(2,1)} %all-gather.9.cloned.1.call-done), kind=kOutput, calls=%fused_computation.19 | convolution fusion | flops 17179869184 | bytes 46137344 | tf_op jit(solution)/shard_map/dot_general | solution.py:38
  105.8 23.4 %all-gather.11.cloned.1.call-done = bf16[2048,1024]{1,0:T(8,128)(2,1)} async-done(((bf16[512,1024]{1,0:T(8,128)(2,1)}), bf16[2048,1024]{1,0:T(8,128)(2,1)}) %all-gather.11.cloned.1.call-update) | async-done | bytes 4194320 | tf_op jit(solution)/shard_map/all_gather | solution.py:29
  129.1 22.6 %all-gather.13.cloned.1.call-done = bf16[1024,4096]{1,0:T(8,128)(2,1)} async-done(((bf16[1024,2048]{1,0:T(8,128)(2,1)}), bf16[1024,4096]{1,0:T(8,128)(2,1)}) %all-gather.13.cloned.1.call-update) | async-done | bytes 8388624 | tf_op jit(solution)/shard_map/all_gather | solution.py:30
  151.7 25.0 %fusion.12 = f32[2048,4096]{1,0:T(8,128)} fusion(bf16[2048,1024]{1,0:T(8,128)(2,1)} %all-gather.11.cloned.1.call-done, bf16[1024,4096]{1,0:T(8,128)(2,1)} %all-gather.13.cloned.1.call-done), kind=kOutput, calls=%fused_computation.20 | convolution fusion | flops 17179869184 | bytes 46137344 | tf_op jit(solution)/shard_map/dot_general | solution.py:31
  176.9 258.8 %reduce-scatter.6.cloned.1.call-done = f32[512,4096]{1,0:T(8,128)} async-done(((f32[2048,4096]{1,0:T(8,128)}), f32[512,4096]{1,0:T(8,128)}) %reduce-scatter.6.cloned.1.call-update) | async-done | bytes 8388624 | tf_op jit(solution)/shard_map/reduce_scatter | solution.py:39
  435.7 282.2 %reduce-scatter.8.cloned.1.call-done = f32[512,4096]{1,0:T(8,128)} async-done(((f32[2048,4096]{1,0:T(8,128)}), f32[512,4096]{1,0:T(8,128)}) %reduce-scatter.8.cloned.1.call-update) | async-done | bytes 8388624 | tf_op jit(solution)/shard_map/reduce_scatter | solution.py:32
  717.9 11.2 fusion.7
  729.3 0.7 all-gather.17.cloned.1.call-update
  730.3 151.1 %all-gather.15.cloned.1.call-done = bf16[2048,4096]{1,0:T(8,128)(2,1)} async-done(((bf16[512,4096]{1,0:T(8,128)(2,1)}), bf16[2048,4096]{1,0:T(8,128)(2,1)}) %all-gather.15.cloned.1.call-update) | async-done | bytes 16777232 | tf_op jit(solution)/shard_map/all_gather | solution.py:44
  881.4 24.1 %fusion.13 = f32[2048,1024]{1,0:T(8,128)} fusion(bf16[2048,4096]{1,0:T(8,128)(2,1)} %all-gather.15.cloned.1.call-done, bf16[1024,4096]{1,0:T(8,128)(2,1)} %all-gather.13.cloned.1.call-done), kind=kOutput, calls=%fused_computation.21 | convolution fusion | flops 17179869184 | bytes 33554432 | tf_op jit(solution)/shard_map/dot_general | solution.py:45
  905.7 23.8 %convolution_bitcast_fusion = f32[1024,4096]{0,1:T(8,128)} fusion(bf16[2048,4096]{1,0:T(8,128)(2,1)} %all-gather.15.cloned.1.call-done, bf16[2048,1024]{1,0:T(8,128)(2,1)} %all-gather.11.cloned.1.call-done), kind=kOutput, calls=%fused_computation.9 | convolution fusion | flops 17179869184 | bytes 37748736 | tf_op jit(solution)/shard_map/dot_general | solution.py:47
  929.8 107.1 %all-gather.17.cloned.1.call-done = bf16[2048,4096]{1,0:T(8,128)(2,1)} async-done(((bf16[512,4096]{1,0:T(8,128)(2,1)}), bf16[2048,4096]{1,0:T(8,128)(2,1)}) %all-gather.17.cloned.1.call-update) | async-done | bytes 16777232 | tf_op jit(solution)/shard_map/all_gather | solution.py:41
  1036.9 23.8 %fusion.14 = f32[4096,1024]{1,0:T(8,128)} fusion(bf16[2048,4096]{1,0:T(8,128)(2,1)} %all-gather.17.cloned.1.call-done, bf16[2048,1024]{1,0:T(8,128)(2,1)} %all-gather.7.cloned.1.call-done), kind=kOutput, calls=%fused_computation.22 | convolution fusion | flops 17179869184 | bytes 37748736 | tf_op jit(solution)/shard_map/dot_general | solution.py:42
  1060.7 57.6 %reduce-scatter.10.cloned.1.call-done = f32[512,1024]{1,0:T(8,128)} async-done(((f32[2048,1024]{1,0:T(8,128)}), f32[512,1024]{1,0:T(8,128)}) %reduce-scatter.10.cloned.1.call-update) | async-done | bytes 2097168 | tf_op jit(solution)/shard_map/reduce_scatter | solution.py:46
  1118.3 2.7 convert_element_type.24
  1121.0 23.7 %reduce-scatter.12.cloned.1.call-done = f32[1024,2048]{0,1:T(8,128)} async-done(((f32[1024,4096]{0,1:T(8,128)}), f32[1024,2048]{0,1:T(8,128)}) %reduce-scatter.12.cloned.1.call-update) | async-done | bytes 8388624 | tf_op jit(solution)/shard_map/reduce_scatter | solution.py:48
  1144.7 6.1 convert_element_type.25
  1150.8 6.4 copy.7
  1157.2 15.9 %reduce-scatter.14.cloned.1.call-done = f32[4096,512]{1,0:T(8,128)} async-done(((f32[4096,1024]{1,0:T(8,128)}), f32[4096,512]{1,0:T(8,128)}) %reduce-scatter.14.cloned.1.call-update) | async-done | bytes 8388624 | tf_op jit(solution)/shard_map/reduce_scatter | solution.py:43
  1173.1 5.9 convert_element_type.27
  (19 shorter events, 2.7 us)
Async XLA Ops:
  7.2 50.5 %all-gather.7.cloned.1.call-start = ((), (), s32[]{:S(2)}) async-start(), calls=%async_computation.5 | async-start | bytes 5242880 | tf_op jit(solution)/shard_map/all_gather | solution.py:36
  8.0 72.5 %all-gather.9.cloned.1.call-start = ((), (), s32[]{:S(2)}) async-start(), calls=%async_computation.6 | async-start | bytes 12582912 | tf_op jit(solution)/shard_map/all_gather | solution.py:37
  8.8 120.4 %all-gather.11.cloned.1.call-start = ((), (), s32[]{:S(2)}) async-start(), calls=%async_computation.8 | async-start | bytes 5242880 | tf_op jit(solution)/shard_map/all_gather | solution.py:29
  9.6 142.2 %all-gather.13.cloned.1.call-start = ((), (), s32[]{:S(2)}) async-start(), calls=%async_computation.9 | async-start | bytes 12582912 | tf_op jit(solution)/shard_map/all_gather | solution.py:30
  10.2 425.5 %reduce-scatter.6.cloned.1.call-start = ((), (), s32[]{:S(2)}) async-start(), calls=%async_computation.7 | async-start | bytes 41943040 | tf_op jit(solution)/shard_map/reduce_scatter | solution.py:39
  105.7 612.2 %reduce-scatter.8.cloned.1.call-start = ((), (), s32[]{:S(2)}) async-start(), calls=%async_computation.10 | async-start | bytes 41943040 | tf_op jit(solution)/shard_map/reduce_scatter | solution.py:32
  176.8 704.6 %all-gather.15.cloned.1.call-start = ((), (), s32[]{:S(2)}) async-start(), calls=%async_computation.11 | async-start | bytes 20971520 | tf_op jit(solution)/shard_map/all_gather | solution.py:44
  729.2 307.7 %all-gather.17.cloned.1.call-start = ((), (), s32[]{:S(2)}) async-start(), calls=%async_computation.14 | async-start | bytes 20971520 | tf_op jit(solution)/shard_map/all_gather | solution.py:41
  730.0 388.2 %reduce-scatter.10.cloned.1.call-start = ((), (), s32[]{:S(2)}) async-start(), calls=%async_computation.12 | async-start | bytes 10485760 | tf_op jit(solution)/shard_map/reduce_scatter | solution.py:46
  905.6 239.1 %reduce-scatter.12.cloned.1.call-start = ((), (), s32[]{:S(2)}) async-start(), calls=%async_computation.13 | async-start | bytes 25165824 | tf_op jit(solution)/shard_map/reduce_scatter | solution.py:48
  929.5 243.6 %reduce-scatter.14.cloned.1.call-start = ((), (), s32[]{:S(2)}) async-start(), calls=%async_computation.15 | async-start | bytes 25165824 | tf_op jit(solution)/shard_map/reduce_scatter | solution.py:43
Sparse Core Ops, SparseCore 0:
  9.6 48.1 all-gather.6
  59.3 21.1 all-gather.8
  82.0 47.0 all-gather.10
  130.5 21.1 all-gather.12
  154.0 281.7 reduce-scatter.5
  437.9 279.9 reduce-scatter.7
  729.3 152.0 all-gather.14
  883.5 153.2 all-gather.16
  1039.2 78.9 reduce-scatter.9
  1120.4 24.2 reduce-scatter.11
  1147.0 26.0 reduce-scatter.13
where the time goes:
time: 1190 us
  waiting for transfers between devices  1020 us (86%)
  matrix products  122 us (10%)
  other arithmetic  26 us (2%)
  between operations  13.9 us (1%)
    reduce_scatter x1, waiting for transfers between devices, local_step(): pre_sum = lax.psum_scatter(pre_part, 'cy', scatter_dimension=0, tiled=True)  282 us
    reduce_scatter x1, waiting for transfers between devices, local_step(): h_grad = lax.psum_scatter(h_part, 'cy', scatter_dimension=0, tiled=True)  259 us
    all_gather x1, waiting for transfers between devices, local_step(): grad_full = lax.all_gather(pre_grad, 'cy', axis=0, tiled=True)  151 us
    all_gather x1, waiting for transfers between devices, local_step(): hidden_full = lax.all_gather(hidden, 'cy', axis=0, tiled=True)  107 us
    reduce_scatter x1, waiting for transfers between devices, local_step(): lax.psum_scatter(x_part, 'cz', scatter_dimension=0, tiled=True)  57.6 us
    all_gather x1, waiting for transfers between devices, local_step(): z_full = lax.all_gather(z_grad, 'cz', axis=0, tiled=True)  47.4 us
    dot_general x1, matrix products, local_step(): lax.dot_general(z_full, down_full, CONTRACT_LAST, preferred_element_type=...  25.2 us
    dot_general x1, matrix products, local_step(): pre_part = jnp.dot(x_full, up_full, preferred_element_type=jnp.float32)  25 us
  transfers between devices with their start and end apart: 11, of which 11 were waited for; matrix products, arithmetic and copies ran while one was open for 12% of the time, Pallas kernels for 0%

commit v1 on v0

v1 whole, which is shorter than its diff:
```python
import math
import jax
import jax.numpy as jnp
from jax import lax
from jax.sharding import PartitionSpec as P

GELU_COEF = 0.044715
SQRT_TWO_PI = math.sqrt(2.0 / math.pi)
CONTRACT_LAST = (((1,), (1,)), ((), ()))
CONTRACT_FIRST = (((0,), (0,)), ((), ()))


def gelu_parts(pre_act):
    inner_arg = SQRT_TWO_PI * (pre_act + GELU_COEF * pre_act * pre_act * pre_act)
    tanh_val = jnp.tanh(inner_arg)
    gelu_val = 0.5 * pre_act * (1.0 + tanh_val)
    gelu_slope = 0.5 * (1.0 + tanh_val) + 0.5 * pre_act * (1.0 - tanh_val * tanh_val) * SQRT_TWO_PI * (1.0 + 3.0 * GELU_COEF * pre_act * pre_act)
    return gelu_val, gelu_slope


def solution(mesh):
    ncx, ncy = mesh.shape["cx"], mesh.shape["cy"]
    row_spec = P(("dp", "cx", "cz"), "cy")
    up_spec = P("cy", ("cz", "cx"))
    down_spec = P("cz", ("cy", "cx"))
    up_out = P(("dp", "cy"), ("cz", "cx"))
    down_out = P(("dp", "cz"), ("cy", "cx"))

    def local_step(x_act, w_up, w_down, z_grad):
        dloc, floc = w_up.shape
        sub = floc // ncy
        x_row = lax.all_gather(x_act, "cy", axis=1, tiled=True)
        x_full = lax.all_gather(x_row, "cz", axis=0, tiled=True)
        g_row = lax.all_gather(z_grad, "cy", axis=1, tiled=True)
        g_full = lax.all_gather(g_row, "cz", axis=0, tiled=True)
        up_slice = lax.all_to_all(w_up, "cy", split_axis=1, concat_axis=0, tiled=True)
        up_slice = lax.all_gather(up_slice, "cx", axis=1, tiled=True)
        wd = w_down.reshape(ncx, ncy, sub, -1).transpose(1, 0, 2, 3).reshape(ncy, ncx * sub, -1)
        wd = lax.all_to_all(wd, "cy", split_axis=0, concat_axis=0)
        wd = lax.all_gather(wd, "cx", axis=1)
        down_slice = wd.transpose(2, 0, 1, 3).reshape(ncx * sub, -1)
        pre_act = jnp.dot(x_full, up_slice, preferred_element_type=jnp.float32).astype(jnp.bfloat16).astype(jnp.float32)
        gelu_val, gelu_slope = gelu_parts(pre_act)
        hidden = gelu_val.astype(jnp.bfloat16)
        h_grad = lax.dot_general(g_full, down_slice, CONTRACT_LAST, preferred_element_type=jnp.float32)
        pre_grad = (h_grad * gelu_slope).astype(jnp.bfloat16)
        grad_all = lax.all_gather(pre_grad, "cy", axis=0)
        rows = grad_all.shape[1]
        grad_full = grad_all.reshape(ncy, rows, ncx, sub).transpose(1, 2, 0, 3).reshape(rows, -1)
        up_full = lax.all_gather(w_up, "cx", axis=1, tiled=True)
        x_part = lax.dot_general(grad_full, up_full, CONTRACT_LAST, preferred_element_type=jnp.float32)
        x_grad = lax.psum_scatter(x_part, "cz", scatter_dimension=0, tiled=True).astype(jnp.bfloat16)
        down_part = lax.dot_general(hidden, g_full, CONTRACT_FIRST, preferred_element_type=jnp.float32)
        down_part = down_part.reshape(ncx * sub, ncy, ncx, -1).transpose(2, 0, 1, 3).reshape(ncx * ncx * sub, -1)
        down_sum = lax.psum_scatter(down_part, "cx", scatter_dimension=0, tiled=True).astype(jnp.bfloat16)
        down_sum = down_sum.reshape(ncx * sub, ncy, -1)
        down_all = lax.all_to_all(down_sum, "cy", split_axis=1, concat_axis=0)
        down_grad = down_all.reshape(ncy, ncx, sub, -1).transpose(1, 0, 2, 3).reshape(ncy * ncx * sub, -1)
        x_col = lax.all_gather(x_act, "cz", axis=0, tiled=True)
        up_part = lax.dot_general(x_col, grad_full, CONTRACT_FIRST, preferred_element_type=jnp.float32)
        up_grad = lax.psum_scatter(up_part, "cx", scatter_dimension=1, tiled=True).astype(jnp.bfloat16)
        return (x_grad, up_grad, down_grad)

    return jax.shard_map(local_step, mesh=mesh, in_specs=(row_spec, up_spec, down_spec, row_spec), out_specs=(row_spec, up_out, down_out), check_vma=False)
```

time: 1190 us -> 960 us (0.81)
  waiting for transfers between devices: 1020 us -> 409 us
  blocking collectives: 0 us -> 225 us
  local copies, waits for them, and re-layouts: 6.42 us -> 162 us
    reduce_scatter x3 -> x1, waiting for transfers between devices: 557 us -> 0.02 us  [local_step(): lax.psum_scatter(down_part, 'cx', scatter_dimension=0, tiled=True)]
    all_to_all x0 -> x3, blocking collectives: none -> 225 us  [the longest x1 86.4 us: local_step(): wd = lax.all_to_all(wd, 'cy', split_axis=0, concat_axis=0)]
    reshape x0 -> x4, local copies, waits for them, and re-layouts: none -> 104 us  [the longest x2 68.8 us: local_step(): grad_all.reshape(ncy, rows, ncx, sub).transpose(1, 2, 0, 3)]
    reduce_scatter x1, waiting for transfers between devices: 57.6 us -> 0.01 us  [local_step(): lax.psum_scatter(x_part, 'cz', scatter_dimension=0, tiled=True)]
    all_gather x5 -> x8, waiting for transfers between devices: 352 us -> 389 us  [the longest x1 155 us: local_step(): x_full = lax.all_gather(x_row, 'cz', axis=0, tiled=True)]
    all_gather x1, waiting for transfers between devices: 22.6 us -> 0.01 us  [local_step(): up_full = lax.all_gather(w_up, 'cx', axis=1, tiled=True)]
    unnamed x1 -> x3, local copies, waits for them, and re-layouts: 6.42 us -> 24 us
  transfers between devices with their start and end apart: 11 -> 12, of which waited for: 11 -> 6; matrix products, arithmetic and copies ran while one was open for 12% -> 28% of each run, Pallas kernels for 0% -> 0%
where the time goes in v1:
time: 960 us; the launch traced here: 954 us
  waiting for transfers between devices  409 us (43%)
  blocking collectives  225 us (23%)
  local copies, waits for them, and re-layouts  162 us (17%)
  matrix products  128 us (13%)
  other arithmetic  14.8 us (2%)
  between operations  14.3 us (1%)
    all_gather x1, waiting for transfers between devices, local_step(): x_full = lax.all_gather(x_row, 'cz', axis=0, tiled=True)  155 us
    all_gather x1, waiting for transfers between devices, local_step(): g_full = lax.all_gather(g_row, 'cz', axis=0, tiled=True)  131 us
    all_to_all x1, blocking collectives, local_step(): wd = lax.all_to_all(wd, 'cy', split_axis=0, concat_axis=0)  86.4 us
    all_to_all x1, blocking collectives, local_step(): lax.all_to_all(w_up, 'cy', split_axis=1, concat_axis=0, tiled=True)  86.2 us
    all_gather x1, waiting for transfers between devices, local_step(): grad_all = lax.all_gather(pre_grad, 'cy', axis=0)  75.6 us
    reshape x2, local copies, waits for them, and re-layouts, local_step(): grad_all.reshape(ncy, rows, ncx, sub).transpose(1, 2, 0, 3)  68.8 us
    all_to_all x1, blocking collectives, local_step(): down_all = lax.all_to_all(down_sum, 'cy', split_axis=1, concat_axis=0)  52.3 us
    reshape x2, local copies, waits for them, and re-layouts, local_step(): down_part.reshape(ncx * sub, ncy, ncx, -1).transpose(2, 0, 1, 3)  35.3 us
  transfers between devices with their start and end apart: 12, of which 6 were waited for; matrix products, arithmetic and copies ran while one was open for 28% of the time, Pallas kernels for 0%

profile of v1, /device:TPU:96, one launch (start us, length us, event | category | flops | bytes accessed | tf_op | source)
XLA Modules:
  0.0 954.4 jit_solution(8712896211039026658)
XLA Ops:
  11.5 86.4 %all_to_all.39 = bf16[4,1024,512]{2,1,0:T(8,128)(2,1)} all-to-all(bf16[4,1024,512]{2,1,0:T(8,128)(2,1)S(1)} %bitcast.44), channel_id=1, replica_groups=mesh['dp'=1,'cz'=4,'cy'=4,'cx'=2] {'cy'}, dimensions={0} | all-to-all | bytes 8388608 | tf_op jit(solution)/shard_map/all_to_all | solution.py:39
  98.0 6.4 copy.24
  104.4 86.2 %all_to_all.40 = bf16[1024,4,512]{0,2,1:T(8,128)(2,1)} all-to-all(bf16[1024,4,512]{0,2,1:T(8,128)(2,1)} %bitcast.45), channel_id=1, replica_groups=mesh['dp'=1,'cz'=4,'cy'=4,'cx'=2] {'cy'}, dimensions={1} | all-to-all | bytes 8388608 | tf_op jit(solution)/shard_map/all_to_all | solution.py:36
  190.7 6.2 copy.25
  198.3 13.6 %all-gather.26.cloned.1.call-done = bf16[4,2048,512]{2,1,0:T(8,128)(2,1)} async-done(((bf16[4,1024,512]{2,1,0:T(8,128)(2,1)}), bf16[4,2048,512]{2,1,0:T(8,128)(2,1)}) %all-gather.26.cloned.1.call-update) | async-done | bytes 8388624 | tf_op jit(solution)/shard_map/all_gather | solution.py:40
  211.8 11.5 %copy.23 = bf16[4,2,1024,512]{2,3,1,0:T(8,128)(2,1)} copy(bf16[4,2,1024,512]{3,2,1,0:T(8,128)(2,1)} %bitcast.46) | data formatting | bytes 16777216 | tf_op jit(solution)/shard_map/all_gather | solution.py:40
  223.3 12.8 %all-gather.20.cloned.1.call-done = bf16[4096,1024]{1,0:T(8,128)(2,1)} async-done(((bf16[4096,512]{1,0:T(8,128)(2,1)}), bf16[4096,1024]{1,0:T(8,128)(2,1)}) %all-gather.20.cloned.1.call-update) | async-done | bytes 8388624 | tf_op jit(solution)/shard_map/all_gather | solution.py:37
  236.2 155.3 %all-gather.18.cloned.1.call-done = bf16[2048,4096]{1,0:T(8,128)(2,1)} async-done(((bf16[512,4096]{1,0:T(8,128)(2,1)}), bf16[2048,4096]{1,0:T(8,128)(2,1)}) %all-gather.18.cloned.1.call-update) | async-done | bytes 16777232 | tf_op jit(solution)/shard_map/all_gather | solution.py:33
  391.5 23.6 %convolution_convert_fusion = bf16[2048,1024]{1,0:T(8,128)(2,1)} fusion(bf16[2048,4096]{1,0:T(8,128)(2,1)} %all-gather.18.cloned.1.call-done, bf16[4096,1024]{1,0:T(8,128)(2,1)} %all-gather.20.cloned.1.call-done), kind=kOutput, calls=%fused_computation.24 | convolution fusion | flops 17181966336 | bytes 29360128 | tf_op jit(solution)/shard_map/dot_general | solution.py:42
  415.1 131.1 %all-gather.14.cloned.1.call-done = bf16[2048,4096]{1,0:T(8,128)(2,1)} async-done(((bf16[512,4096]{1,0:T(8,128)(2,1)}), bf16[2048,4096]{1,0:T(8,128)(2,1)}) %all-gather.14.cloned.1.call-update) | async-done | bytes 16777232 | tf_op jit(solution)/shard_map/all_gather | solution.py:35
  546.2 27.9 %fusion.6 = bf16[2048,1024]{1,0:T(8,128)(2,1)} fusion(bf16[2048,1024]{1,0:T(8,128)(2,1)} %convolution_convert_fusion, bf16[2048,4096]{1,0:T(8,128)(2,1)} %all-gather.14.cloned.1.call-done, bf16[1024,4096]{0,1:T(8,128)(2,1)} %bitcast.47), kind=kOutput, calls=%fused_computation.14 | convolution fusion | flops 17221812224 | bytes 33554432 | tf_op jit(solution)/shard_map/dot_general | solution.py:45
  576.0 29.2 %fusion.11 = f32[1024,4096]{1,0:T(8,128)} fusion(bf16[2048,4096]{1,0:T(8,128)(2,1)} %all-gather.14.cloned.1.call-done, bf16[2048,1024]{1,0:T(8,128)(2,1)} %convolution_convert_fusion), kind=kOutput, calls=%fused_computation.19 | convolution fusion | flops 17200840704 | bytes 37748736 | tf_op jit(solution)/shard_map/dot_general | solution.py:53
  605.2 22.0 %reshape.39 = f32[1024,4,2,512]{3,2,1,0:T(2,128)} reshape(f32[1024,4096]{1,0:T(8,128)} %fusion.11) | data formatting | bytes 33554432 | tf_op jit(solution)/shard_map/reshape | solution.py:54
  627.2 13.3 %copy.27 = f32[1024,4,2,512]{3,1,0,2:T(4,128)S(1)} copy(f32[1024,4,2,512]{3,2,1,0:T(2,128)} %reshape.39) | data formatting | bytes 33554432 | tf_op jit(solution)/shard_map/reshape | solution.py:54
  640.5 11.1 %copy.31 = f32[256,8,4,512]{3,1,2,0:T(8,128)} copy(f32[256,8,4,512]{3,2,1,0:T(4,128)S(1)} %bitcast.38) | data formatting | bytes 33554432
  652.0 75.6 %all-gather.28.cloned.1.call-done = bf16[8192,1024]{1,0:T(8,128)(2,1)} async-done(((bf16[2048,1024]{1,0:T(8,128)(2,1)}), bf16[8192,1024]{1,0:T(8,128)(2,1)}) %all-gather.28.cloned.1.call-update) | async-done | bytes 16777232 | tf_op jit(solution)/shard_map/all_gather | solution.py:47
  727.6 27.7 %reshape.37 = bf16[4,2048,2,512]{3,2,1,0:T(2,128)(2,1)} reshape(bf16[8192,1024]{1,0:T(8,128)(2,1)} %all-gather.28.cloned.1.call-done) | data formatting | bytes 33554432 | tf_op jit(solution)/shard_map/reshape | solution.py:49
  755.4 41.0 %copy.26 = bf16[4,2048,2,512]{1,3,0,2:T(8,128)(2,1)} copy(bf16[4,2048,2,512]{3,2,1,0:T(2,128)(2,1)} %reshape.37) | data formatting | bytes 33554432 | tf_op jit(solution)/shard_map/reshape | solution.py:49
  796.4 24.3 %fusion.21 = f32[2048,1024]{1,0:T(8,128)} fusion(bf16[2048,4096]{0,1:T(8,128)(2,1)} %bitcast.39, bf16[1024,4096]{1,0:T(8,128)(2,1)} %all-gather.22.cloned.1.call-done), kind=kOutput, calls=%fused_computation.29 | convolution fusion | flops 17179869184 | bytes 33554432 | tf_op jit(solution)/shard_map/dot_general | solution.py:51
  820.8 23.4 %convolution_bitcast_fusion = f32[1024,4096]{0,1:T(8,128)} fusion(bf16[2048,4096]{0,1:T(8,128)(2,1)} %bitcast.40, bf16[2048,1024]{1,0:T(8,128)(2,1)} %all-gather.24.cloned.1.call-done), kind=kOutput, calls=%fused_computation.9 | convolution fusion | flops 17179869184 | bytes 37748736 | tf_op jit(solution)/shard_map/dot_general | solution.py:60
  850.4 7.8 broadcast_in_dim_reshape.3
  861.2 52.3 %all_to_all.41 = bf16[1,1024,4,512]{3,1,0,2:T(8,128)(2,1)S(1)} all-to-all(bf16[1,1024,4,512]{3,1,0,2:T(8,128)(2,1)S(1)} %copy.28), channel_id=1, replica_groups=mesh['dp'=1,'cz'=4,'cy'=4,'cx'=2] {'cy'}, dimensions={2} | all-to-all | bytes 8388608 | tf_op jit(solution)/shard_map/all_to_all | solution.py:57
  918.7 16.4 %reduce-scatter.6.cloned.1.call-done = f32[1024,2048]{0,1:T(8,128)} async-done(((f32[1024,4096]{0,1:T(8,128)}), f32[1024,2048]{0,1:T(8,128)}) %reduce-scatter.6.cloned.1.call-update) | async-done | bytes 8388624 | tf_op jit(solution)/shard_map/reduce_scatter | solution.py:61
  941.1 6.4 copy.30
  (36 shorter events, 28.5 us)
Async XLA Ops:
  7.2 189.8 %all-gather.16.cloned.1.call-start = ((), (), s32[]{:S(2)}) async-start(), calls=%async_computation.8 | async-start | bytes 5242880 | tf_op jit(solution)/shard_map/all_gather | solution.py:32
  8.0 189.7 %all-gather.12.cloned.1.call-start = ((), (), s32[]{:S(2)}) async-start(), calls=%async_computation.6 | async-start | bytes 5242880 | tf_op jit(solution)/shard_map/all_gather | solution.py:34
  8.8 203.1 %all-gather.26.cloned.1.call-start = ((), (), s32[]{:S(2)}) async-start(), calls=%async_computation.16 | async-start | bytes 12582912 | tf_op jit(solution)/shard_map/all_gather | solution.py:40
  97.9 138.2 %all-gather.20.cloned.1.call-start = ((), (), s32[]{:S(2)}) async-start(), calls=%async_computation.10 | async-start | bytes 12582912 | tf_op jit(solution)/shard_map/all_gather | solution.py:37
  196.9 194.6 %all-gather.18.cloned.1.call-start = ((), (), s32[]{:S(2)}) async-start(), calls=%async_computation.9 | async-start | bytes 20971520 | tf_op jit(solution)/shard_map/all_gather | solution.py:33
  197.6 348.7 %all-gather.14.cloned.1.call-start = ((), (), s32[]{:S(2)}) async-start(), calls=%async_computation.7 | async-start | bytes 20971520 | tf_op jit(solution)/shard_map/all_gather | solution.py:35
  198.2 529.4 %all-gather.28.cloned.1.call-start = ((), (), s32[]{:S(2)}) async-start(), calls=%async_computation.17 | async-start | bytes 20971520 | tf_op jit(solution)/shard_map/all_gather | solution.py:47
  574.2 222.2 %all-gather.22.cloned.1.call-start = ((), (), s32[]{:S(2)}) async-start(), calls=%async_computation.11 | async-start | bytes 12582912 | tf_op jit(solution)/shard_map/all_gather | solution.py:50
  575.0 245.8 %all-gather.24.cloned.1.call-start = ((), (), s32[]{:S(2)}) async-start(), calls=%async_computation.13 | async-start | bytes 5242880 | tf_op jit(solution)/shard_map/all_gather | solution.py:59
  575.8 268.5 %reduce-scatter.8.cloned.1.call-start = ((), (), s32[]{:S(2)}) async-start(), calls=%async_computation.15 | async-start | bytes 25165824 | tf_op jit(solution)/shard_map/reduce_scatter | solution.py:55
  651.7 264.3 %reduce-scatter.4.cloned.1.call-start = ((), (), s32[]{:S(2)}) async-start(), calls=%async_computation.12 | async-start | bytes 10485760 | tf_op jit(solution)/shard_map/reduce_scatter | solution.py:52
  820.7 114.4 %reduce-scatter.6.cloned.1.call-start = ((), (), s32[]{:S(2)}) async-start(), calls=%async_computation.14 | async-start | bytes 25165824 | tf_op jit(solution)/shard_map/reduce_scatter | solution.py:61
Sparse Core Ops, SparseCore 0:
  9.6 87.8 all-gather.15
  99.0 91.1 all-gather.11
  191.8 19.9 all-gather.25
  213.8 22.2 all-gather.19
  237.6 153.8 all-gather.17
  392.9 153.2 all-gather.13
  574.3 153.2 all-gather.27
  729.2 21.7 all-gather.21
  752.5 47.0 all-gather.23
  801.8 24.9 reduce-scatter.7
  829.1 79.5 reduce-scatter.3
  910.8 24.2 reduce-scatter.5

commit v2 on v0

v2 whole, which is shorter than its diff:
```python
import functools
import math

import jax
import jax.numpy as jnp
from jax import lax
from jax.experimental import pallas as pl
from jax.experimental.pallas import tpu as pltpu
from jax.sharding import PartitionSpec as P

GELU_COEF = 0.044715
SQRT_TWO_PI = math.sqrt(2.0 / math.pi)
NN = (((1,), (0,)), ((), ()))
NT = (((1,), (1,)), ((), ()))
TN = (((0,), (0,)), ((), ()))
MESH = pl.DeviceIdType.MESH
RING = 4
CORES = 2
PAN = 3
GROUPS = ((0, 0, 8), (1, 0, 8), (2, 0, 8), (3, 0, 4), (3, 4, 4))
NB = 4
NG = len(GROUPS)
EARLY = 2
X, G = 0, 1


def gelu_parts(pre_act):
    inner_arg = SQRT_TWO_PI * (pre_act + GELU_COEF * pre_act * pre_act * pre_act)
    tanh_val = jnp.tanh(inner_arg)
    gelu_val = 0.5 * pre_act * (1.0 + tanh_val)
    gelu_slope = 0.5 * (1.0 + tanh_val) + 0.5 * pre_act * (1.0 - tanh_val * tanh_val) * SQRT_TWO_PI * (1.0 + 3.0 * GELU_COEF * pre_act * pre_act)
    return gelu_val, gelu_slope


(XS, XR, W2, W1, WR, CS, CR, O2, O1, OR, YA, YB, YF, YR, Q2, QD, QS, WN, WP, GP, XP, HP, CP,
 OWN, L1, L2, L3, L4, L5, LX, LH, M1, M2, M3, M4, M5, QA, QF, OUT) = range(39)
PANEL_OF = {L1: M1, L2: M2, L3: M3, L4: M4, L5: M5}
O5 = (2, 0, 1, 3)
O4 = (0, 1, 2, 3)


def full(a, r):
    return [(XS, a, r), (XR, a, r), (YR, a, r), (OWN, 0, 0)] + ([(YA, a, r), (YB, a, r)] if r < EARLY else [(YF, a, r)])


def make_plan():
    it, un = {}, {}
    groups = range(NG)
    for r in groups:
        q = GROUPS[r][2] / 8 / NB
        f = 4 * q
        for a in (X, G):
            it[XS, a, r] = (0, q, [])
            it[XR, a, r] = (0, q / 2, [(XS, a, r)])
            row = [(XS, a, r), (XR, a, r)]
            if r < EARLY:
                it[YA, a, r] = (1, q, [])
                it[YB, a, r] = (1, 3 * q, row)
                it[YR, a, r] = (1, 2 * q, [(YA, a, r), (YB, a, r)])
            else:
                it[YF, a, r] = (1, 4 * q, row + [(OWN, 0, 0)])
                it[YR, a, r] = (1, 2 * q, [(YF, a, r)])
        it[GP, 0, r] = (2, 8 * q, full(G, r))
        it[XP, 0, r] = (2, 4 * q, full(X, r))
        it[HP, 0, r] = (2, 4 * q, [(M2, 0, r)])
        it[CS, 0, r] = (0, 4 * q, [(M2, 0, r)])
        it[CR, 0, r] = (0, 2 * q, [(CS, 0, r)])
        dc = [(CS, 0, r), (CR, 0, r)]
        it[CP, 0, r] = (2, 8 * q, dc)
        it[Q2, 0, r] = (1, q, [(M3, 0, r)])
        it[QD, 0, r] = (1, q, [(M3, 0, r)])
        it[QS, 0, r] = (1, q, [(QA, 0, r)])
        it[L1, 0, r] = (3, 16 * q, full(X, r))
        it[L2, 0, r] = (3, 16 * q, full(G, r))
        it[L3, 0, r] = (3, 16 * q, dc)
        wu = [(WP, 0, p) for p in range(3)]
        wd = [(WP, 1, p) for p in range(3)]
        un[M1, 0, r] = (0.4 + 4.4 * f, [(L1, 0, r)] + wu)
        un[M2, 0, r] = (0.4 + 6.2 * f, [(L2, 0, r), (M1, 0, r)] + wd)
        un[M3, 0, r] = (0.4 + 4.4 * f, [(L3, 0, r), (WN, 0, 0)] + ([(QF, 0, r - 2)] if r >= 2 else []))
        un[QA, 0, r] = (0.1 + 0.4 * f, [(Q2, 0, r)])
        un[QF, 0, r] = (0.1 + 0.4 * f, [(QS, 0, r), (QD, 0, r)])
    for w in range(2):
        it[W2, 0, w] = (0, 0.5, [])
        it[W1, 0, w] = (0, 1.0, [])
        it[WR, 0, w] = (0, 0.5, [(W2, 0, w)])
        it[WP, w, 0] = (2, 1, [])
        it[WP, w, 1] = (2, 2, [(W1, 0, w)])
        it[WP, w, 2] = (2, 1, [(WR, 0, w)])
    it[WN, 0, 0] = (2, 4, [])
    it[OWN, 0, 0] = (3, 2, [])
    it[O2, 0, 0] = (0, 0.5, [(M5, 0, 0)])
    it[O1, 0, 0] = (0, 1.0, [(M5, 0, 1)])
    it[OR, 0, 0] = (0, 0.5, [(O2, 0, 0)])
    for p in range(RING):
        it[L5, 0, p] = (3, 4, [(GP, 0, r) for r in groups] + sum([full(G, r) for r in groups], []))
        it[L4, 0, p] = (3, 4, [(CP, 0, r) for r in groups] + [(CR, 0, r) for r in groups])
    it[LH, 0, 0] = (3, 4, [(HP, 0, r) for r in groups] + [(M2, 0, r) for r in groups])
    it[LX, 0, 0] = (3, 8, [(XP, 0, r) for r in groups] + [(M1, 0, r) for r in groups])
    for p in range(2):
        un[M5, 0, p] = (9.6, [(L5, 0, 2 * p), (L5, 0, 2 * p + 1), (LH, 0, 0)])
        un[M4, 0, p] = (9.6, [(L4, 0, 2 * p), (L4, 0, 2 * p + 1), (LX, 0, 0), (M5, 0, 0), (M5, 0, 1)])
    return it, un


def make_lists():
    over_cy = [
        (XS, 0, 0), (XS, 1, 1), (XR, 0, 0), (XS, 0, 1), (XR, 1, 1), (XS, 1, 2), (XS, 0, 3), (XS, 1, 0), (XS, 0, 2),
        (XR, 0, 1), (XR, 1, 2), (XR, 1, 0), (W2, 0, 0), (W1, 0, 1), (W2, 0, 1), (W1, 0, 0), (XR, 0, 2), (WR, 0, 0),
        (WR, 0, 1), (XS, 1, 4), (XS, 1, 3), (XS, 0, 4), (XR, 1, 4), (XR, 0, 3), (XR, 1, 3), (CS, 0, 0), (CS, 0, 1),
        (XR, 0, 4), (CR, 0, 0), (CS, 0, 2), (CR, 0, 1), (CS, 0, 3), (CR, 0, 2), (CR, 0, 3), (CS, 0, 4), (O2, 0, 0),
        (CR, 0, 4), (OR, 0, 0), (O1, 0, 0),
    ]
    over_cz = [
        (YA, 1, 0), (YA, 1, 1), (YA, 0, 0), (YA, 0, 1), (YB, 0, 0), (YB, 1, 1), (YR, 0, 0), (YB, 0, 1), (YB, 1, 0),
        (YR, 0, 1), (YR, 1, 0), (YF, 1, 2), (YR, 1, 1), (YF, 0, 2), (YR, 1, 2), (YR, 0, 2), (YF, 1, 3), (YF, 0, 3),
        (YR, 1, 3), (YR, 0, 3), (YF, 0, 4), (YF, 1, 4), (YR, 0, 4), (YR, 1, 4), (Q2, 0, 1), (Q2, 0, 0), (QD, 0, 0),
        (QS, 0, 0), (QS, 0, 1), (QD, 0, 1), (Q2, 0, 2), (QD, 0, 2), (QS, 0, 2), (Q2, 0, 4), (Q2, 0, 3), (QD, 0, 3),
        (QS, 0, 3), (QS, 0, 4), (QD, 0, 4),
    ]
    units = [
        (QF, 0, 3), (QA, 0, 0), (M3, 0, 1), (M4, 0, 0), (M5, 0, 0), (M1, 0, 0), (M2, 0, 0), (QA, 0, 2), (QF, 0, 0),
        (QF, 0, 4), (M3, 0, 2), (M3, 0, 0), (M4, 0, 1), (QF, 0, 2), (M2, 0, 2), (M1, 0, 2), (M1, 0, 1), (M2, 0, 3),
        (M2, 0, 1), (M5, 0, 1), (M1, 0, 4), (M3, 0, 3), (M3, 0, 4), (M2, 0, 4), (QA, 0, 1), (QF, 0, 1), (M1, 0, 3),
        (QA, 0, 4), (QA, 0, 3),
    ]
    return [over_cy, over_cz], units


RATE = (22.5, 22.5, 1.7, 0.4)
DELAY = (3.0, 3.0, 1.5, 1.5)


def make_order(plan, lists, units):
    it, un = plan
    done, free, pos = {}, [0.0] * 4, [0] * 4
    pend, now, order, panels, waits = list(units), 0.0, [], [], []
    late = [n for n in it if it[n][0] >= 2]
    rank = {u: i for i, u in enumerate(units)}
    panel_rank = lambda n: rank[PANEL_OF[n[0]], 0, n[2] // 2 if n[0] in (L4, L5) else n[2]] if n[0] in PANEL_OF else -1
    through = lambda n: (PANEL_OF[n[0]], 0, n[2] // 2 if n[0] in (L4, L5) else n[2]) in gone
    gone = set()
    big = 1e9

    def ready(n):
        return all(done.get(d, big) <= now for d in it[n][2])

    def send(n):
        k = it[n][0]
        start = max(now + 0.3, free[k])
        waits.append((k, start - free[k], n))
        free[k] = start + it[n][1] * RATE[k]
        done[n] = free[k] + DELAY[k]
        order.append(n)

    while True:
        for k in (0, 1):
            while pos[k] < len(lists[k]) and ready(lists[k][pos[k]]):
                send(lists[k][pos[k]])
                pos[k] += 1
        for n in sorted((n for n in late if ready(n)), key=lambda n: (panel_rank(n), n)):
            if n[0] in PANEL_OF:
                if len(panels) >= PAN and not through(panels[-PAN]):
                    continue
                panels.append(n)
            late.remove(n)
            send(n)
        can = [u for u in pend if all(done.get(d, big) <= now for d in un[u][1])]
        if can:
            pend.remove(can[0])
            order.append(can[0])
            now += un[can[0]][0]
            done[can[0]] = now
            gone.add(can[0])
            continue
        later = [v for v in done.values() if v > now]
        if not later:
            break
        now = min(later)
    assert not pend and not late and all(pos[k] == len(lists[k]) for k in (0, 1)), (pend, late, pos)
    return order, panels, max(done.values()), waits


class Copies:
    def __init__(self, send, recv, local, peers):
        self.send, self.recv, self.local, self.peers = send, recv, local, peers
        self.n_remote = self.n_local = 0
        self.by_name = {}

    def add(self, name, pairs):
        made = []
        for src, dst, to in pairs:
            if to is None:
                c = pltpu.make_async_copy(src, dst, self.local.at[self.n_local])
                self.n_local += 1
            else:
                axis, idx = self.peers[to]
                c = pltpu.make_async_remote_copy(
                    src, dst, self.send.at[self.n_remote], self.recv.at[self.n_remote],
                    device_id={axis: idx}, device_id_type=MESH)
                self.n_remote += 1
            made.append([c, to, False, False])
            c.start()
        self.by_name.setdefault(name, []).extend(made)

    def arrived(self, name):
        for m in self.by_name.get(name, ()):
            if not m[2]:
                m[2] = True
                m[0].wait() if m[1] is None else m[0].wait_recv()

    def left(self, name):
        for m in self.by_name.get(name, ()):
            if m[1] is None:
                if not m[2]:
                    m[2] = True
                    m[0].wait()
            elif not m[3]:
                m[3] = True
                m[0].wait_send()

    def finish(self):
        for name in list(self.by_name):
            self.arrived(name)
            self.left(name)


N_REMOTE = 196
N_LOCAL = 80


def kernel(plan, order, panels, xa, wu, wd, za, dx, dwu, dwd, XF, GF, DF, GPB, DPB, XPB, HPB, su, sd, sw,
           wus, wds, wun, hbuf, pan, ft, dct, rst, rrc, obuf, xo, acc, send, recv, local):
    it, un = plan
    x, y, c = lax.axis_index("cy"), lax.axis_index("cz"), lax.axis_index("cx")
    peers = {
        "R": ("cy", lax.rem(x + 1, RING)), "L": ("cy", lax.rem(x + RING - 1, RING)),
        "U": ("cz", lax.rem(y + 1, RING)), "N": ("cz", lax.rem(y + RING - 1, RING)),
        "P": ("cx", 1 - c),
    }
    barrier = pltpu.get_barrier_semaphore()
    for axis, idx in peers.values():
        pl.semaphore_signal(barrier, inc=1, device_id={axis: idx}, device_id_type=MESH)
    pl.semaphore_wait(barrier, len(peers))

    cp = Copies(send, recv, local, peers)
    blk_rows = xa.shape[1]
    sub = wd.shape[2]
    dh = wu.shape[1]
    mine = pl.ds(pl.multiple_of(c * sub, sub), sub)
    theirs = pl.ds(pl.multiple_of((1 - c) * sub, sub), sub)
    lo, hi = pl.ds(0, sub), pl.ds(sub, sub)
    at = lambda j: lax.rem(x + j, RING)
    cols = lambda j: pl.ds(pl.multiple_of(at(j) * sub, sub), sub)
    slot_of = {n: i % PAN for i, n in enumerate(panels)}
    inp, buf = (xa, za), (XF, GF)

    def group(r):
        b, first, n = GROUPS[r]
        unit_rows = blk_rows // 8
        return b, first * unit_rows, n * unit_rows

    def rel(r, k, part=None):
        _, first, n = group(r)
        start = RING * first + k * n
        return pl.ds(start, n) if part is None else pl.ds(start + part * (n // 2), n // 2)

    def span(r):
        _, first, n = group(r)
        return pl.ds(RING * first, RING * n)

    def copies_of(name):
        kind, a, r = name
        both = lambda right, left: [right + ("R",), left + ("L",)]
        updn = lambda up, down: [up + ("U",), down + ("N",)]
        if kind == WN:
            return sum([[(wu.at[:, :, cols(j)], wun.at[2 * j:2 * j + 2, :, mine], to) for to in (None, "P")] for j in range(RING)], [])
        if kind == XS or kind == YA:
            b, first, n = group(r)
            src = inp[a].at[b, pl.ds(first, n)]
            if kind == XS:
                return both((src, buf[a].at[3, b, rel(r, 0)]), (src, buf[a].at[1, b, rel(r, 0)]))
            return updn((src, buf[a].at[0, b, rel(r, 3)]), (src, buf[a].at[0, b, rel(r, 1)]))
        if kind == XR:
            b, f, s = group(r)[0], rel(r, 0, 0), rel(r, 0, 1)
            return both((buf[a].at[3, b, f], buf[a].at[2, b, f]), (buf[a].at[1, b, s], buf[a].at[2, b, s]))
        if kind in (YB, YF):
            b, m = group(r)[0], buf[a]
            js = pl.ds(1, RING - 1) if kind == YB else pl.ds(0, RING)
            return updn((m.at[js, b, rel(r, 0)], m.at[js, b, rel(r, 3)]), (m.at[js, b, rel(r, 0)], m.at[js, b, rel(r, 1)]))
        if kind == YR:
            b, m = group(r)[0], buf[a]
            return updn((m.at[0:2, b, rel(r, 3)], m.at[0:2, b, rel(r, 2)]), (m.at[2:4, b, rel(r, 1)], m.at[2:4, b, rel(r, 2)]))
        if kind in (W2, W1, WR):
            half = (lambda h, j: wu.at[h, :, cols(j)]) if r == 0 else (lambda h, j: wd.at[h, at(j)])
            piece = (lambda j: wu.at[:, :, cols(j)]) if r == 0 else (lambda j: wd.at[:, at(j)])
            st, dst = (su, sd)[r], (wus, wds)[r]
            if kind == W2:
                return both((half(0, 2), st.at[0]), (half(1, 2), st.at[1]))
            if kind == W1:
                return both((piece(1), dst.at[6:8, :, mine]), (piece(3), dst.at[2:4, :, mine]))
            return both((st.at[0], dst.at[4, :, mine]), (st.at[1], dst.at[5, :, mine]))
        if kind == WP:
            m = (wus, wds)[a]
            if r == 0:
                src = wu.at[:, :, cols(0)] if a == 0 else wd.at[:, at(0)]
                return [(src, m.at[0:2, :, mine], to) for to in (None, "P")]
            return [(m.at[2 * j:2 * j + 2, :, mine], m.at[2 * j:2 * j + 2, :, mine], "P") for j in ((1, 3) if r == 1 else (2,))]
        if kind == GP:
            return [(GF.at[:, group(r)[0], span(r), theirs], GPB.at[:, group(r)[0], span(r)], "P")]
        if kind == XP:
            return [(XF.at[0, group(r)[0], span(r)], XPB.at[group(r)[0], span(r)], "P")]
        if kind == HP:
            return [(hbuf.at[group(r)[0], span(r)], HPB.at[group(r)[0], span(r)], "P")]
        if kind == CP:
            return [(DF.at[:, group(r)[0], span(r), theirs], DPB.at[:, group(r)[0], span(r)], "P")]
        if kind == CS:
            b, _, n = group(r)
            s = dct.at[r % 2, pl.ds(0, RING * n)]
            return both((s, DF.at[3, b, span(r)]), (s, DF.at[1, b, span(r)])) + [(s, DF.at[0, b, span(r)], None)]
        if kind == CR:
            b, first, n = group(r)
            f, s = (pl.ds(RING * first + h * 2 * n, 2 * n) for h in range(2))
            return both((DF.at[3, b, f], DF.at[2, b, f]), (DF.at[1, b, s], DF.at[2, b, s]))
        if kind in (Q2, QD, QS):
            b, first, n = group(r)
            f = ft.at[r % 2]
            own = lambda k: pl.ds(k * n, n)
            rs = pl.ds(first, n)
            if kind == Q2:
                return updn((f.at[0, own(2)], rst.at[b, 0, rs]), (f.at[1, own(2)], rst.at[b, 1, rs]))
            if kind == QD:
                return updn((f.at[1, own(1)], rrc.at[b, 0, 1, rs]), (f.at[0, own(3)], rrc.at[b, 1, 0, rs]))
            return updn((f.at[0, own(1)], rrc.at[b, 0, 0, rs]), (f.at[1, own(3)], rrc.at[b, 1, 1, rs]))
        if kind in (L1, L2, L3):
            b, _, n = group(r)
            m = {L1: XF, L2: GF, L3: DF}[kind]
            return [(m.at[:, b, span(r)], pan.at[slot_of[name], :, pl.ds(0, RING * n)], None)]
        if kind in (L5, L4):
            m, p, j = (GF, GPB, O5[r]) if kind == L5 else (DF, DPB, O4[r])
            s = pan.at[slot_of[name]]
            return [(m.at[j, :, :, mine], s.at[:, :, lo], None), (p.at[j], s.at[:, :, hi], None)]
        if kind == LH:
            return [(HPB, wds.at[0:4], None)]
        if kind == LX:
            return [(XF.at[0], wus.at[0:4], None), (XPB, wus.at[4:8], None)]
        place = {j: i for i, j in enumerate(O5)}
        if kind == O2:
            return both((obuf.at[place[2], 0], sw.at[0]), (obuf.at[place[2], 1], sw.at[1]))
        if kind == O1:
            return both((obuf.at[place[1]], dwd.at[:, x]), (obuf.at[place[3]], dwd.at[:, x]))
        assert kind == OR
        return both((sw.at[0], dwd.at[0, at(3)]), (sw.at[1], dwd.at[1, at(1)]))

    def total(terms):
        out = None
        for a, b, dims in terms:
            d = lax.dot_general(a, b, dims, preferred_element_type=jnp.float32)
            out = d if out is None else out + d
        return out

    def loop(n, body):
        def step(i, carry):
            body(i)
            return carry
        lax.fori_loop(0, n, step, 0)

    def unit(name):
        kind, _, r = name
        if kind in (M1, M2, M3):
            b, first, n = group(r)
            rows = pl.ds(0, RING * n)
        if kind == M1:
            p = pan.at[slot_of[L1, 0, r]]

            def body(t):
                ns = pl.ds(pl.multiple_of(t * sub, sub), sub)
                s = total([(p[j, rows, h * dh:(h + 1) * dh], wus[2 * j + h, :, ns], NN) for j in range(RING) for h in range(2)])
                hbuf[b, span(r), ns] = s.astype(jnp.bfloat16)
            loop(2, body)
        elif kind == M2:
            p = pan.at[slot_of[L2, 0, r]]
            if r >= 2:
                cp.left((CS, 0, r - 2))
            d = dct.at[r % 2]
            step = min(32, RING * n)

            def body(t):
                ns = pl.ds(pl.multiple_of(t * sub, sub), sub)
                acc[rows, :] = total([(p[j, rows, :], wds[2 * j + t], NT) for j in range(RING)])

                def elem(e):
                    rs = pl.ds(pl.multiple_of(e * step, step), step)
                    hs = pl.ds(pl.multiple_of(RING * first + e * step, step), step)
                    g, s = gelu_parts(hbuf[b, hs, ns].astype(jnp.float32))
                    hbuf[b, hs, ns] = g.astype(jnp.bfloat16)
                    d[rs, ns] = (acc[rs, :] * s).astype(jnp.bfloat16)
                loop(RING * n // step, elem)
            loop(2, body)
        elif kind == M3:
            p = pan.at[slot_of[L3, 0, r]]
            if r >= 2:
                for q in (Q2, QD, QS):
                    cp.left((q, 0, r - 2))
            f = ft.at[r % 2]

            def body(t):
                f[t, rows, :] = total([(p[j, rows, :], wun[2 * j + t], NT) for j in range(RING)])
            loop(2, body)
        elif kind in (M5, M4):
            ld = L5 if kind == M5 else L4
            s0, s1 = slot_of[ld, 0, 2 * r], slot_of[ld, 0, 2 * r + 1]
            own, par = (hbuf, wds) if kind == M5 else (wus, wus.at[4:8])
            if kind == M4 and r == 0:
                for g in range(NG):
                    cp.left((HP, 0, g))

            def body(i):
                e, t = i // 2, lax.rem(i, 2)
                p = pan.at[s0 + e * (s1 - s0)]
                ms = pl.ds(pl.multiple_of(t * dh, dh), dh)
                s = total([(own[g, :, ms], p[g, :, lo], TN) for g in range(NB)] + [(par[g, :, ms], p[g, :, hi], TN) for g in range(NB)])
                if kind == M5:
                    obuf[2 * r + e, t] = s.astype(jnp.bfloat16)
                else:
                    hbuf[2 * r + e, :, ms] = s.astype(jnp.bfloat16)
            loop(4, body)
            for e in range(2):
                i = 2 * r + e
                if kind == M5 and O5[i] == 0:
                    cp.add((OUT, kind, i), [(obuf.at[i], dwd.at[:, x], None)])
                if kind == M4:
                    cp.add((OUT, kind, i), [(hbuf.at[i, :, h * dh:(h + 1) * dh], dwu.at[h, :, cols(O4[i])], None) for h in range(2)])
        else:
            b, first, n = group(r)
            f = ft.at[r % 2]
            rs = pl.ds(first, n)
            own = lambda k: pl.ds(k * n, n)
            if kind == QA:
                f[0, own(1), :] = f[0, own(1), :] + rst[b, 0, rs, :]
                f[1, own(3), :] = f[1, own(3), :] + rst[b, 1, rs, :]
            else:
                for h in range(2):
                    xo[b, rs, h * dh:(h + 1) * dh] = (f[h, own(0), :] + rrc[b, 0, h, rs, :] + rrc[b, 1, h, rs, :]).astype(jnp.bfloat16)
                cp.add((OUT, kind, r), [(xo.at[b, rs], dx.at[b, rs], None)])

    for name in order:
        for d in (it[name][2] if name in it else un[name][1]):
            cp.arrived(d)
        if name[0] == OWN:
            own = pl.ds(0, blk_rows)
            b0, b1 = pan.at[0, :, own], pan.at[1, :, own]
            cp.add((OUT, OWN, 0), [(xa, b0, None), (za, b1, None)])
            cp.arrived((OUT, OWN, 0))
            pairs = []
            for r in range(NG):
                b, first, n = group(r)
                pairs += [(pan.at[a, b, pl.ds(first, n)], buf[a].at[0, b, rel(r, 0)], None) for a in (X, G)]
            cp.add(name, pairs)
        elif name in it:
            for w in {LX: (0,), LH: (1,)}.get(name[0], ()):
                for p in range(3):
                    cp.left((WP, w, p))
            cp.add(name, copies_of(name))
        else:
            unit(name)
    cp.finish()
    assert cp.n_remote <= N_REMOTE and cp.n_local <= N_LOCAL, (cp.n_remote, cp.n_local)


def solution(mesh):
    assert mesh.shape["cy"] == RING and mesh.shape["cz"] == RING and mesh.shape["cx"] == CORES
    row_spec = P(("dp", "cx", "cz"), "cy")
    up_spec = P("cy", ("cz", "cx"))
    down_spec = P("cz", ("cy", "cx"))
    up_out = P(("dp", "cy"), ("cz", "cx"))
    down_out = P(("dp", "cz"), ("cy", "cx"))
    plan = make_plan()
    order, panels, _, _ = make_order(plan, *make_lists())

    def local_step(x_act, w_up, w_down, z_grad):
        t_loc, d_loc = x_act.shape
        f_loc = w_up.shape[1]
        rows, sub, dh = t_loc // NB, f_loc // RING, d_loc // 2
        grp = RING * rows
        bf, f32 = jnp.bfloat16, jnp.float32
        xa, za = x_act.reshape(NB, rows, d_loc), z_grad.reshape(NB, rows, d_loc)
        wu = w_up.reshape(2, dh, f_loc)
        wd = w_down.reshape(CORES, RING, sub, dh)
        hbm = lambda *s: jax.ShapeDtypeStruct(s, bf)
        outs = (
            hbm(NB, rows, d_loc), hbm(2, dh, f_loc), hbm(CORES, RING, sub, dh),
            hbm(RING, NB, grp, d_loc), hbm(RING, NB, grp, d_loc), hbm(RING, NB, grp, 2 * sub),
            hbm(RING, NB, grp, sub), hbm(RING, NB, grp, sub), hbm(NB, grp, d_loc), hbm(NB, grp, 2 * sub),
            hbm(2, dh, sub), hbm(2, sub, dh), hbm(2, sub, dh),
        )
        scratch = [
            pltpu.VMEM((2 * RING, dh, 2 * sub), bf), pltpu.VMEM((2 * RING, sub, d_loc), bf), pltpu.VMEM((2 * RING, dh, 2 * sub), bf),
            pltpu.VMEM((NB, grp, 2 * sub), bf), pltpu.VMEM((PAN, RING, grp, d_loc), bf),
            pltpu.VMEM((2, 2, grp, dh), f32), pltpu.VMEM((2, grp, 2 * sub), bf),
            pltpu.VMEM((NB, 2, rows, dh), f32), pltpu.VMEM((NB, 2, 2, rows, dh), f32),
            pltpu.VMEM((RING, CORES, sub, dh), bf), pltpu.VMEM((NB, rows, d_loc), bf),
            pltpu.VMEM((grp, sub), f32),
            pltpu.SemaphoreType.DMA((N_REMOTE,)), pltpu.SemaphoreType.DMA((N_REMOTE,)), pltpu.SemaphoreType.DMA((N_LOCAL,)),
        ]
        any_spec = pl.BlockSpec(memory_space=pl.ANY)
        res = pl.pallas_call(
            functools.partial(kernel, plan, order, panels),
            out_shape=outs,
            in_specs=[any_spec] * 4,
            out_specs=[any_spec] * len(outs),
            scratch_shapes=scratch,
            compiler_params=pltpu.CompilerParams(collective_id=0, has_side_effects=True, vmem_limit_bytes=67043328),
            name="mlp_bwd",
        )(xa, wu, wd, za)
        return (res[0].reshape(t_loc, d_loc), res[1].reshape(w_up.shape), res[2].reshape(w_down.shape))

    return jax.shard_map(local_step, mesh=mesh, in_specs=(row_spec, up_spec, down_spec, row_spec), out_specs=(row_spec, up_out, down_out), check_vma=False)
```

time: 1190 us -> 370 us (0.31)
  waiting for transfers between devices: 1020 us -> 0 us
  Pallas kernels: 0 us -> 359 us
  matrix products: 122 us -> 0 us
  other arithmetic: 26 us -> 0 us
  between operations: 13.9 us -> 0.64 us
    reduce_scatter x5 -> x0, waiting for transfers between devices: 638 us -> none  [the longest x1 282 us: local_step(): pre_sum = lax.psum_scatter(pre_part, 'cy', scatter_dimension=0, tiled=True)]
    all_gather x6 -> x0, waiting for transfers between devices: 374 us -> none  [the longest x1 151 us: local_step(): grad_full = lax.all_gather(pre_grad, 'cy', axis=0, tiled=True)]
    pallas_call x0 -> x1, Pallas kernels: none -> 359 us  [local_step(): pl.pallas_call(functools.partial(kernel, plan, order, panels), out_shape=...]
    dot_general x5 -> x0, matrix products: 122 us -> none  [the longest x1 25.2 us: local_step(): lax.dot_general(z_full, down_full, CONTRACT_LAST, preferred_element_type=...]
    convert_element_type x4 -> x0, other arithmetic: 26 us -> none  [the longest x1 11.2 us: local_step(): hidden = gelu_val.astype(jnp.bfloat16)]
  transfers between devices with their start and end apart: 11 -> 0, of which waited for: 11 -> 0; matrix products, arithmetic and copies ran while one was open for 12% -> 0% of each run, Pallas kernels for 0% -> 0%
where the time goes in v2:
time: 370 us; the launch traced here: 368 us
  Pallas kernels  359 us (97%)
  local copies, waits for them, and re-layouts  9.22 us (2%)
    pallas_call x1, Pallas kernels, local_step(): pl.pallas_call(functools.partial(kernel, plan, order, panels), out_shape=...  359 us
    unnamed x5, local copies, waits for them, and re-layouts  9.22 us

profile of v2, /device:TPU:96, one launch (start us, length us, event | category | flops | bytes accessed | tf_op | source)
XLA Modules:
  0.0 368.5 jit_solution(13892535983090618091)
XLA Ops:
  0.6 358.6 %mlp_bwd.1 = (bf16[4,128,1024]{2,1,0:T(8,128)(2,1)}, bf16[2,512,2048]{2,1,0:T(8,128)(2,1)}, bf16[2,4,512,512]{3,2,1,0:T(8,128)(2,1)}, bf16[4,4,512,1024]{3,2,1,0...) custom-call(bf16[4,128,1024]{2,1,0:T(8,128)(2,1)} %bitcast.11, ...), custom_call_target="tpu_custom_call" | custom-call | tf_op jit(solution)/shard_map/mlp_bwd/pallas_call | solution.py:507
  359.3 2.3 copy.10
  361.5 0.0 copy-start
  361.5 4.9 %copy.11 = bf16[1024,2048]{1,0:T(8,128)(2,1)} copy(bf16[1024,2048]{1,0:T(8,128)(2,1)} %bitcast.10) | data formatting | bytes 8388608
  366.5 0.0 copy-done
  366.5 2.0 copy.12
Async XLA Ops:
  361.5 4.9 %copy-start = (bf16[2,4,512,512]{3,2,1,0:T(8,128)(2,1)S(1)}, bf16[2,4,512,512]{3,2,1,0:T(8,128)(2,1)}, u32[]{:S(2)}) copy-start(bf16[2,4,512,512]{3,2,1,0:T(8,128)(2,1)} %get-tuple-element.8) | copy-start | bytes 12582916

commit v3 on v2

--- a/solution.py
+++ b/solution.py
@@ -1,5 +1,6 @@
 import functools
 import math
+import string
 
 import jax
 import jax.numpy as jnp
@@ -35,12 +36,11 @@
 (XS, XR, W2, W1, WR, CS, CR, O2, O1, OR, YA, YB, YF, YR, Q2, QD, QS, WN, WP, GP, XP, HP, CP,
  OWN, L1, L2, L3, L4, L5, LX, LH, M1, M2, M3, M4, M5, QA, QF, OUT) = range(39)
 PANEL_OF = {L1: M1, L2: M2, L3: M3, L4: M4, L5: M5}
-O5 = (2, 0, 1, 3)
-O4 = (0, 1, 2, 3)
+O5 = (2, 1, 3, 0)
 
 
 def full(a, r):
-    return [(XS, a, r), (XR, a, r), (YR, a, r), (OWN, 0, 0)] + ([(YA, a, r), (YB, a, r)] if r < EARLY else [(YF, a, r)])
+    return [(XS, a, r), (XR, a, r), (YR, a, r), (OWN,)] + ([(YA, a, r), (YB, a, r)] if r < EARLY else [(YF, a, r)])
 
 
 def make_plan():
@@ -58,74 +58,80 @@
                 it[YB, a, r] = (1, 3 * q, row)
                 it[YR, a, r] = (1, 2 * q, [(YA, a, r), (YB, a, r)])
             else:
-                it[YF, a, r] = (1, 4 * q, row + [(OWN, 0, 0)])
+                it[YF, a, r] = (1, 4 * q, row + [(OWN,)])
                 it[YR, a, r] = (1, 2 * q, [(YF, a, r)])
-        it[GP, 0, r] = (2, 8 * q, full(G, r))
-        it[XP, 0, r] = (2, 4 * q, full(X, r))
-        it[HP, 0, r] = (2, 4 * q, [(M2, 0, r)])
-        it[CS, 0, r] = (0, 4 * q, [(M2, 0, r)])
-        it[CR, 0, r] = (0, 2 * q, [(CS, 0, r)])
-        dc = [(CS, 0, r), (CR, 0, r)]
-        it[CP, 0, r] = (2, 8 * q, dc)
-        it[Q2, 0, r] = (1, q, [(M3, 0, r)])
-        it[QD, 0, r] = (1, q, [(M3, 0, r)])
-        it[QS, 0, r] = (1, q, [(QA, 0, r)])
-        it[L1, 0, r] = (3, 16 * q, full(X, r))
-        it[L2, 0, r] = (3, 16 * q, full(G, r))
-        it[L3, 0, r] = (3, 16 * q, dc)
+        it[GP, r] = (2, 8 * q, full(G, r))
+        it[XP, r] = (2, 4 * q, full(X, r))
+        it[HP, r] = (2, 4 * q, [(M2, r)])
+        it[CS, r] = (0, 4 * q, [(M2, r)])
+        it[CR, r] = (0, 2 * q, [(CS, r)])
+        dc = [(CS, r), (CR, r)]
+        it[CP, r] = (2, 8 * q, dc)
+        it[Q2, r] = (1, q, [(M3, r)])
+        it[QD, r] = (1, q, [(M3, r)])
+        it[QS, r] = (1, q, [(QA, r)])
+        it[L1, r] = (3, 16 * q, full(X, r))
+        it[L2, r] = (3, 16 * q, full(G, r))
+        it[L3, r] = (3, 16 * q, dc)
         wu = [(WP, 0, p) for p in range(3)]
         wd = [(WP, 1, p) for p in range(3)]
-        un[M1, 0, r] = (0.4 + 4.4 * f, [(L1, 0, r)] + wu)
-        un[M2, 0, r] = (0.4 + 6.2 * f, [(L2, 0, r), (M1, 0, r)] + wd)
-        un[M3, 0, r] = (0.4 + 4.4 * f, [(L3, 0, r), (WN, 0, 0)] + ([(QF, 0, r - 2)] if r >= 2 else []))
-        un[QA, 0, r] = (0.1 + 0.4 * f, [(Q2, 0, r)])
-        un[QF, 0, r] = (0.1 + 0.4 * f, [(QS, 0, r), (QD, 0, r)])
+        un[M1, r] = (0.4 + 4.4 * f, [(L1, r)] + wu)
+        un[M2, r] = (0.4 + 6.2 * f, [(L2, r), (M1, r)] + wd)
+        un[M3, r] = (0.4 + 4.4 * f, [(L3, r), (WN,)] + ([(QF, r - 2)] if r >= 2 else []))
+        un[QA, r] = (0.1 + 0.4 * f, [(Q2, r)])
+        un[QF, r] = (0.1 + 0.4 * f, [(QS, r), (QD, r)])
     for w in range(2):
-        it[W2, 0, w] = (0, 0.5, [])
-        it[W1, 0, w] = (0, 1.0, [])
-        it[WR, 0, w] = (0, 0.5, [(W2, 0, w)])
+        it[W2, w] = (0, 0.5, [])
+        it[W1, w] = (0, 1.0, [])
+        it[WR, w] = (0, 0.5, [(W2, w)])
         it[WP, w, 0] = (2, 1, [])
-        it[WP, w, 1] = (2, 2, [(W1, 0, w)])
-        it[WP, w, 2] = (2, 1, [(WR, 0, w)])
-    it[WN, 0, 0] = (2, 4, [])
-    it[OWN, 0, 0] = (3, 2, [])
-    it[O2, 0, 0] = (0, 0.5, [(M5, 0, 0)])
-    it[O1, 0, 0] = (0, 1.0, [(M5, 0, 1)])
-    it[OR, 0, 0] = (0, 0.5, [(O2, 0, 0)])
+        it[WP, w, 1] = (2, 2, [(W1, w)])
+        it[WP, w, 2] = (2, 1, [(WR, w)])
+    it[(WN,)] = (2, 4, [])
+    it[(OWN,)] = (3, 2, [])
+    it[(O2,)] = (0, 0.5, [(M5, 0)])
+    it[(O1,)] = (0, 1.0, [(M5, 1), (M5, 2)])
+    it[(OR,)] = (0, 0.5, [(O2,)])
     for p in range(RING):
-        it[L5, 0, p] = (3, 4, [(GP, 0, r) for r in groups] + sum([full(G, r) for r in groups], []))
-        it[L4, 0, p] = (3, 4, [(CP, 0, r) for r in groups] + [(CR, 0, r) for r in groups])
-    it[LH, 0, 0] = (3, 4, [(HP, 0, r) for r in groups] + [(M2, 0, r) for r in groups])
-    it[LX, 0, 0] = (3, 8, [(XP, 0, r) for r in groups] + [(M1, 0, r) for r in groups])
+        it[L5, p] = (3, 4, [(GP, r) for r in groups] + sum([full(G, r) for r in groups], []))
+        it[L4, p] = (3, 4, [(CP, r) for r in groups] + [(CR, r) for r in groups])
+    it[(LH,)] = (3, 4, [(HP, r) for r in groups] + [(M2, r) for r in groups])
+    it[(LX,)] = (3, 8, [(XP, r) for r in groups] + [(M1, r) for r in groups])
+    for p in range(RING):
+        un[M5, p] = (4.9, [(L5, p), (LH,)])
     for p in range(2):
-        un[M5, 0, p] = (9.6, [(L5, 0, 2 * p), (L5, 0, 2 * p + 1), (LH, 0, 0)])
-        un[M4, 0, p] = (9.6, [(L4, 0, 2 * p), (L4, 0, 2 * p + 1), (LX, 0, 0), (M5, 0, 0), (M5, 0, 1)])
+        un[M4, p] = (9.6, [(L4, 2 * p), (L4, 2 * p + 1), (LX,)])
     return it, un
 
 
-def make_lists():
-    over_cy = [
-        (XS, 0, 0), (XS, 1, 1), (XR, 0, 0), (XS, 0, 1), (XR, 1, 1), (XS, 1, 2), (XS, 0, 3), (XS, 1, 0), (XS, 0, 2),
-        (XR, 0, 1), (XR, 1, 2), (XR, 1, 0), (W2, 0, 0), (W1, 0, 1), (W2, 0, 1), (W1, 0, 0), (XR, 0, 2), (WR, 0, 0),
-        (WR, 0, 1), (XS, 1, 4), (XS, 1, 3), (XS, 0, 4), (XR, 1, 4), (XR, 0, 3), (XR, 1, 3), (CS, 0, 0), (CS, 0, 1),
-        (XR, 0, 4), (CR, 0, 0), (CS, 0, 2), (CR, 0, 1), (CS, 0, 3), (CR, 0, 2), (CR, 0, 3), (CS, 0, 4), (O2, 0, 0),
-        (CR, 0, 4), (OR, 0, 0), (O1, 0, 0),
+def make_lists(keys=None):
+    xs = lambda r: [(XS, X, r), (XS, G, r), (XR, X, r), (XR, G, r)]
+    w = lambda i: [(W2, i), (W1, i), (WR, i)]
+    y = lambda r: [(YF, X, r), (YF, G, r), (YR, X, r), (YR, G, r)]
+    cs, cr = lambda r: [(CS, r)], lambda r: [(CR, r)]
+    q = lambda r: [(Q2, r), (QD, r), (QS, r)]
+    rest = range(4, NG)
+    lists = [
+        xs(0) + xs(1) + w(0) + xs(2) + w(1) + sum([xs(r) for r in range(3, NG)], []) + cs(0) + cs(1) + cr(0) + cr(1) + cs(2) + cr(2)
+        + sum([cs(r) for r in range(3, NG)], []) + sum([cr(r) for r in range(3, NG)], []) + [(O2,), (O1,), (OR,)],
+        [(YA, X, 0), (YA, G, 0), (YA, X, 1), (YA, G, 1), (YB, X, 0), (YB, G, 0), (YR, X, 0), (YR, G, 0), (YB, X, 1), (YB, G, 1), (YR, X, 1), (YR, G, 1)]
+        + sum([y(r) for r in range(2, NG)], []) + sum([q(r) for r in range(NG)], []),
     ]
-    over_cz = [
-        (YA, 1, 0), (YA, 1, 1), (YA, 0, 0), (YA, 0, 1), (YB, 0, 0), (YB, 1, 1), (YR, 0, 0), (YB, 0, 1), (YB, 1, 0),
-        (YR, 0, 1), (YR, 1, 0), (YF, 1, 2), (YR, 1, 1), (YF, 0, 2), (YR, 1, 2), (YR, 0, 2), (YF, 1, 3), (YF, 0, 3),
-        (YR, 1, 3), (YR, 0, 3), (YF, 0, 4), (YF, 1, 4), (YR, 0, 4), (YR, 1, 4), (Q2, 0, 1), (Q2, 0, 0), (QD, 0, 0),
-        (QS, 0, 0), (QS, 0, 1), (QD, 0, 1), (Q2, 0, 2), (QD, 0, 2), (QS, 0, 2), (Q2, 0, 4), (Q2, 0, 3), (QD, 0, 3),
-        (QS, 0, 3), (QS, 0, 4), (QD, 0, 4),
-    ]
-    units = [
-        (QF, 0, 3), (QA, 0, 0), (M3, 0, 1), (M4, 0, 0), (M5, 0, 0), (M1, 0, 0), (M2, 0, 0), (QA, 0, 2), (QF, 0, 0),
-        (QF, 0, 4), (M3, 0, 2), (M3, 0, 0), (M4, 0, 1), (QF, 0, 2), (M2, 0, 2), (M1, 0, 2), (M1, 0, 1), (M2, 0, 3),
-        (M2, 0, 1), (M5, 0, 1), (M1, 0, 4), (M3, 0, 3), (M3, 0, 4), (M2, 0, 4), (QA, 0, 1), (QF, 0, 1), (M1, 0, 3),
-        (QA, 0, 4), (QA, 0, 3),
-    ]
-    return [over_cy, over_cz], units
-
+    units = []
+    for r in range(NG):
+        units += [(M2, r), (M1, r)]
+    units += [(QA, r) for r in range(NG)] + [(QF, r) for r in range(NG)]
+    units += [(M3, 0), (M3, 1)] + [(M5, p) for p in range(RING)] + [(M3, r) for r in range(2, NG)] + [(M4, 0), (M4, 1)]
+    if keys is not None:
+        lists[0], lists[1], units = ([base[string.ascii_letters.index(ch)] for ch in key] for base, key in zip(lists[:2] + [units], keys))
+    return lists, units
+
+
+ORDER = (
+    "tafcewhbgpdlvixnjyrkqmsozAuBCDEGIFHKJLM",
+    "abdcejfrhglimknopqtsuvwxyBzACDEFGHKJIML",
+    "BmhownAsbpEjrlayvqDkcxdtgfCziue",
+)
 
 RATE = (22.5, 22.5, 1.7, 0.4)
 DELAY = (3.0, 3.0, 1.5, 1.5)
@@ -137,8 +143,8 @@
     pend, now, order, panels, waits = list(units), 0.0, [], [], []
     late = [n for n in it if it[n][0] >= 2]
     rank = {u: i for i, u in enumerate(units)}
-    panel_rank = lambda n: rank[PANEL_OF[n[0]], 0, n[2] // 2 if n[0] in (L4, L5) else n[2]] if n[0] in PANEL_OF else -1
-    through = lambda n: (PANEL_OF[n[0]], 0, n[2] // 2 if n[0] in (L4, L5) else n[2]) in gone
+    user = lambda n: (PANEL_OF[n[0]], n[1] // 2 if n[0] == L4 else n[1])
+    panel_rank = lambda n: rank[user(n)] if n[0] in PANEL_OF else -1
     gone = set()
     big = 1e9
 
@@ -160,7 +166,7 @@
                 pos[k] += 1
         for n in sorted((n for n in late if ready(n)), key=lambda n: (panel_rank(n), n)):
             if n[0] in PANEL_OF:
-                if len(panels) >= PAN and not through(panels[-PAN]):
+                if len(panels) >= PAN and user(panels[-PAN]) not in gone:
                     continue
                 panels.append(n)
             late.remove(n)
@@ -230,7 +236,7 @@
 
 
 def kernel(plan, order, panels, xa, wu, wd, za, dx, dwu, dwd, XF, GF, DF, GPB, DPB, XPB, HPB, su, sd, sw,
-           wus, wds, wun, hbuf, pan, ft, dct, rst, rrc, obuf, xo, acc, send, recv, local):
+           wus, wds, wun, hbuf, pan, ft, dct, rst, rrc, obuf, acc, send, recv, local):
     it, un = plan
     x, y, c = lax.axis_index("cy"), lax.axis_index("cz"), lax.axis_index("cx")
     peers = {
@@ -270,7 +276,7 @@
         return pl.ds(RING * first, RING * n)
 
     def copies_of(name):
-        kind, a, r = name
+        kind, a, r = name[0], name[-2:][0], name[-1]
         both = lambda right, left: [right + ("R",), left + ("L",)]
         updn = lambda up, down: [up + ("U",), down + ("N",)]
         if kind == WN:
@@ -337,7 +343,7 @@
             m = {L1: XF, L2: GF, L3: DF}[kind]
             return [(m.at[:, b, span(r)], pan.at[slot_of[name], :, pl.ds(0, RING * n)], None)]
         if kind in (L5, L4):
-            m, p, j = (GF, GPB, O5[r]) if kind == L5 else (DF, DPB, O4[r])
+            m, p, j = (GF, GPB, O5[r]) if kind == L5 else (DF, DPB, r)
             s = pan.at[slot_of[name]]
             return [(m.at[j, :, :, mine], s.at[:, :, lo], None), (p.at[j], s.at[:, :, hi], None)]
         if kind == LH:
@@ -366,12 +372,12 @@
         lax.fori_loop(0, n, step, 0)
 
     def unit(name):
-        kind, _, r = name
+        kind, r = name[0], name[-1]
         if kind in (M1, M2, M3):
             b, first, n = group(r)
             rows = pl.ds(0, RING * n)
         if kind == M1:
-            p = pan.at[slot_of[L1, 0, r]]
+            p = pan.at[slot_of[L1, r]]
 
             def body(t):
                 ns = pl.ds(pl.multiple_of(t * sub, sub), sub)
@@ -379,9 +385,9 @@
                 hbuf[b, span(r), ns] = s.astype(jnp.bfloat16)
             loop(2, body)
         elif kind == M2:
-            p = pan.at[slot_of[L2, 0, r]]
+            p = pan.at[slot_of[L2, r]]
             if r >= 2:
-                cp.left((CS, 0, r - 2))
+                cp.left((CS, r - 2))
             d = dct.at[r % 2]
             step = min(32, RING * n)
 
@@ -398,39 +404,35 @@
                 loop(RING * n // step, elem)
             loop(2, body)
         elif kind == M3:
-            p = pan.at[slot_of[L3, 0, r]]
+            p = pan.at[slot_of[L3, r]]
             if r >= 2:
                 for q in (Q2, QD, QS):
-                    cp.left((q, 0, r - 2))
+                    cp.left((q, r - 2))
             f = ft.at[r % 2]
 
             def body(t):
                 f[t, rows, :] = total([(p[j, rows, :], wun[2 * j + t], NT) for j in range(RING)])
             loop(2, body)
-        elif kind in (M5, M4):
-            ld = L5 if kind == M5 else L4
-            s0, s1 = slot_of[ld, 0, 2 * r], slot_of[ld, 0, 2 * r + 1]
-            own, par = (hbuf, wds) if kind == M5 else (wus, wus.at[4:8])
-            if kind == M4 and r == 0:
-                for g in range(NG):
-                    cp.left((HP, 0, g))
+        elif kind == M5:
+            p = pan.at[slot_of[L5, r]]
+
+            def body(t):
+                ms = pl.ds(pl.multiple_of(t * dh, dh), dh)
+                s = total([(hbuf[g, :, ms], p[g, :, lo], TN) for g in range(NB)] + [(wds[g, :, ms], p[g, :, hi], TN) for g in range(NB)])
+                obuf[r, t] = s.astype(jnp.bfloat16)
+            loop(2, body)
+            if O5[r] == 0:
+                cp.add((OUT, kind, r), [(obuf.at[r], dwd.at[:, x], None)])
+        elif kind == M4:
+            s0, s1 = slot_of[L4, 2 * r], slot_of[L4, 2 * r + 1]
 
             def body(i):
                 e, t = i // 2, lax.rem(i, 2)
                 p = pan.at[s0 + e * (s1 - s0)]
                 ms = pl.ds(pl.multiple_of(t * dh, dh), dh)
-                s = total([(own[g, :, ms], p[g, :, lo], TN) for g in range(NB)] + [(par[g, :, ms], p[g, :, hi], TN) for g in range(NB)])
-                if kind == M5:
-                    obuf[2 * r + e, t] = s.astype(jnp.bfloat16)
-                else:
-                    hbuf[2 * r + e, :, ms] = s.astype(jnp.bfloat16)
+                s = total([(wus[g, :, ms], p[g, :, lo], TN) for g in range(NB)] + [(wus[NB + g, :, ms], p[g, :, hi], TN) for g in range(NB)])
+                dwu[t, :, cols(2 * r + e)] = s.astype(jnp.bfloat16)
             loop(4, body)
-            for e in range(2):
-                i = 2 * r + e
-                if kind == M5 and O5[i] == 0:
-                    cp.add((OUT, kind, i), [(obuf.at[i], dwd.at[:, x], None)])
-                if kind == M4:
-                    cp.add((OUT, kind, i), [(hbuf.at[i, :, h * dh:(h + 1) * dh], dwu.at[h, :, cols(O4[i])], None) for h in range(2)])
         else:
             b, first, n = group(r)
             f = ft.at[r % 2]
@@ -441,8 +443,7 @@
                 f[1, own(3), :] = f[1, own(3), :] + rst[b, 1, rs, :]
             else:
                 for h in range(2):
-                    xo[b, rs, h * dh:(h + 1) * dh] = (f[h, own(0), :] + rrc[b, 0, h, rs, :] + rrc[b, 1, h, rs, :]).astype(jnp.bfloat16)
-                cp.add((OUT, kind, r), [(xo.at[b, rs], dx.at[b, rs], None)])
+                    dx[b, rs, h * dh:(h + 1) * dh] = (f[h, own(0), :] + rrc[b, 0, h, rs, :] + rrc[b, 1, h, rs, :]).astype(jnp.bfloat16)
 
     for name in order:
         for d in (it[name][2] if name in it else un[name][1]):
@@ -450,8 +451,8 @@
         if name[0] == OWN:
             own = pl.ds(0, blk_rows)
             b0, b1 = pan.at[0, :, own], pan.at[1, :, own]
-            cp.add((OUT, OWN, 0), [(xa, b0, None), (za, b1, None)])
-            cp.arrived((OUT, OWN, 0))
+            cp.add((OUT, OWN), [(xa, b0, None), (za, b1, None)])
+            cp.arrived((OUT, OWN))
             pairs = []
             for r in range(NG):
                 b, first, n = group(r)
@@ -476,7 +477,7 @@
     up_out = P(("dp", "cy"), ("cz", "cx"))
     down_out = P(("dp", "cz"), ("cy", "cx"))
     plan = make_plan()
-    order, panels, _, _ = make_order(plan, *make_lists())
+    order, panels, _, _ = make_order(plan, *make_lists(ORDER))
 
     def local_step(x_act, w_up, w_down, z_grad):
         t_loc, d_loc = x_act.shape
@@ -489,7 +490,7 @@
         wd = w_down.reshape(CORES, RING, sub, dh)
         hbm = lambda *s: jax.ShapeDtypeStruct(s, bf)
         outs = (
-            hbm(NB, rows, d_loc), hbm(2, dh, f_loc), hbm(CORES, RING, sub, dh),
+            pltpu.VMEM((NB, rows, d_loc), bf), pltpu.VMEM((2, dh, f_loc), bf), hbm(CORES, RING, sub, dh),
             hbm(RING, NB, grp, d_loc), hbm(RING, NB, grp, d_loc), hbm(RING, NB, grp, 2 * sub),
             hbm(RING, NB, grp, sub), hbm(RING, NB, grp, sub), hbm(NB, grp, d_loc), hbm(NB, grp, 2 * sub),
             hbm(2, dh, sub), hbm(2, sub, dh), hbm(2, sub, dh),
@@ -499,7 +500,7 @@
             pltpu.VMEM((NB, grp, 2 * sub), bf), pltpu.VMEM((PAN, RING, grp, d_loc), bf),
             pltpu.VMEM((2, 2, grp, dh), f32), pltpu.VMEM((2, grp, 2 * sub), bf),
             pltpu.VMEM((NB, 2, rows, dh), f32), pltpu.VMEM((NB, 2, 2, rows, dh), f32),
-            pltpu.VMEM((RING, CORES, sub, dh), bf), pltpu.VMEM((NB, rows, d_loc), bf),
+            pltpu.VMEM((RING, CORES, sub, dh), bf),
             pltpu.VMEM((grp, sub), f32),
             pltpu.SemaphoreType.DMA((N_REMOTE,)), pltpu.SemaphoreType.DMA((N_REMOTE,)), pltpu.SemaphoreType.DMA((N_LOCAL,)),
         ]
@@ -508,9 +509,9 @@
             functools.partial(kernel, plan, order, panels),
             out_shape=outs,
             in_specs=[any_spec] * 4,
-            out_specs=[any_spec] * len(outs),
+            out_specs=[pl.BlockSpec(memory_space=pltpu.VMEM)] * 2 + [any_spec] * (len(outs) - 2),
             scratch_shapes=scratch,
-            compiler_params=pltpu.CompilerParams(collective_id=0, has_side_effects=True, vmem_limit_bytes=67043328),
+            compiler_params=pltpu.CompilerParams(collective_id=0, has_side_effects=True, vmem_limit_bytes=61800000),
             name="mlp_bwd",
         )(xa, wu, wd, za)
         return (res[0].reshape(t_loc, d_loc), res[1].reshape(w_up.shape), res[2].reshape(w_down.shape))

time: 370 us -> 365 us (0.986)
  no operation moved by 1% of the time
where the time goes in v3:
time: 365 us
  Pallas kernels  357 us (98%)
  local copies, waits for them, and re-layouts  6.69 us (2%)
    pallas_call x1, Pallas kernels, local_step(): pl.pallas_call(functools.partial(kernel, plan, order, panels), out_shape=...  357 us

profile of v3, /device:TPU:96, one launch (start us, length us, event | category | flops | bytes accessed | tf_op | source)
XLA Modules:
  0.0 364.6 jit_solution(16238254985210730371)
XLA Ops:
  0.6 357.2 %mlp_bwd.1 = (bf16[4,128,1024]{2,1,0:T(8,128)(2,1)S(1)}, bf16[2,512,2048]{2,1,0:T(8,128)(2,1)S(1)}, bf16[2,4,512,512]{3,2,1,0:T(8,128)(2,1)}, bf16[4,4,512,1024]...) custom-call(bf16[4,128,1024]{2,1,0:T(8,128)(2,1)} %bitcast.12, ...), custom_call_target="tpu_custom_call" | custom-call | tf_op jit(solution)/shard_map/mlp_bwd/pallas_call | solution.py:508
  357.9 1.0 copy.10
  358.9 0.0 copy-start
  358.9 2.1 copy.11
  361.0 1.6 copy-done
  362.6 2.0 copy.12
Async XLA Ops:
  358.9 3.7 %copy-start = (bf16[2,4,512,512]{3,2,1,0:T(8,128)(2,1)S(1)}, bf16[2,4,512,512]{3,2,1,0:T(8,128)(2,1)}, u32[]{:S(2)}) copy-start(bf16[2,4,512,512]{3,2,1,0:T(8,128)(2,1)} %get-tuple-element.8) | copy-start | bytes 12582916

commit v4 on v3

--- a/solution.py
+++ b/solution.py
@@ -33,10 +33,13 @@
     return gelu_val, gelu_slope
 
 
-(XS, XR, W2, W1, WR, CS, CR, O2, O1, OR, YA, YB, YF, YR, Q2, QD, QS, WN, WP, GP, XP, HP, CP,
- OWN, L1, L2, L3, L4, L5, LX, LH, M1, M2, M3, M4, M5, QA, QF, OUT) = range(39)
+(XS, XR, W2, W1, WR, CS, CR, O2, O1, OR, YA, YB, YF, YR, Q2, QD, QS, WN, WP, GP, XP, HP, CP, CF,
+ OWN, L1, L2, L3, L4, L5, LX, LH, M1, M2, M3, M4, M5, QA, QF, OUT) = range(40)
 PANEL_OF = {L1: M1, L2: M2, L3: M3, L4: M4, L5: M5}
 O5 = (2, 1, 3, 0)
+O4 = (0, 1, 3, 2)
+PARTS = ((0, 1), (1, 2), (3, 1))
+PART_OF = (0, 1, 1, 2)
 
 
 def full(a, r):
@@ -66,7 +69,8 @@
         it[CS, r] = (0, 4 * q, [(M2, r)])
         it[CR, r] = (0, 2 * q, [(CS, r)])
         dc = [(CS, r), (CR, r)]
-        it[CP, r] = (2, 8 * q, dc)
+        it[CP, r] = (2, 6 * q, [(CS, r)])
+        it[CF, r] = (2, 2 * q, [(CR, r)])
         it[Q2, r] = (1, q, [(M3, r)])
         it[QD, r] = (1, q, [(M3, r)])
         it[QS, r] = (1, q, [(QA, r)])
@@ -90,48 +94,32 @@
     it[(WN,)] = (2, 4, [])
     it[(OWN,)] = (3, 2, [])
     it[(O2,)] = (0, 0.5, [(M5, 0)])
-    it[(O1,)] = (0, 1.0, [(M5, 1), (M5, 2)])
+    it[(O1,)] = (0, 1.0, [(M5, 1)])
     it[(OR,)] = (0, 0.5, [(O2,)])
     for p in range(RING):
         it[L5, p] = (3, 4, [(GP, r) for r in groups] + sum([full(G, r) for r in groups], []))
-        it[L4, p] = (3, 4, [(CP, r) for r in groups] + [(CR, r) for r in groups])
+        it[L4, p] = (3, 4, [(CF if O4[p] == 2 else CP, r) for r in groups] + [(CR if O4[p] == 2 else CS, r) for r in groups])
     it[(LH,)] = (3, 4, [(HP, r) for r in groups] + [(M2, r) for r in groups])
-    it[(LX,)] = (3, 8, [(XP, r) for r in groups] + [(M1, r) for r in groups])
-    for p in range(RING):
-        un[M5, p] = (4.9, [(L5, p), (LH,)])
-    for p in range(2):
-        un[M4, p] = (9.6, [(L4, 2 * p), (L4, 2 * p + 1), (LX,)])
+    it[(LX,)] = (3, 8, [(XP, r) for r in groups] + [(M5, 0)])
+    for p, (first, n) in enumerate(PARTS):
+        un[M4, p] = (4.8 * n, [(L4, first + i) for i in range(n)] + [(LX,)])
+        un[M5, p] = (4.8 * n, [(L5, first + i) for i in range(n)] + [(LH,)])
     return it, un
 
 
-def make_lists(keys=None):
-    xs = lambda r: [(XS, X, r), (XS, G, r), (XR, X, r), (XR, G, r)]
-    w = lambda i: [(W2, i), (W1, i), (WR, i)]
-    y = lambda r: [(YF, X, r), (YF, G, r), (YR, X, r), (YR, G, r)]
-    cs, cr = lambda r: [(CS, r)], lambda r: [(CR, r)]
-    q = lambda r: [(Q2, r), (QD, r), (QS, r)]
-    rest = range(4, NG)
-    lists = [
-        xs(0) + xs(1) + w(0) + xs(2) + w(1) + sum([xs(r) for r in range(3, NG)], []) + cs(0) + cs(1) + cr(0) + cr(1) + cs(2) + cr(2)
-        + sum([cs(r) for r in range(3, NG)], []) + sum([cr(r) for r in range(3, NG)], []) + [(O2,), (O1,), (OR,)],
-        [(YA, X, 0), (YA, G, 0), (YA, X, 1), (YA, G, 1), (YB, X, 0), (YB, G, 0), (YR, X, 0), (YR, G, 0), (YB, X, 1), (YB, G, 1), (YR, X, 1), (YR, G, 1)]
-        + sum([y(r) for r in range(2, NG)], []) + sum([q(r) for r in range(NG)], []),
-    ]
-    units = []
-    for r in range(NG):
-        units += [(M2, r), (M1, r)]
-    units += [(QA, r) for r in range(NG)] + [(QF, r) for r in range(NG)]
-    units += [(M3, 0), (M3, 1)] + [(M5, p) for p in range(RING)] + [(M3, r) for r in range(2, NG)] + [(M4, 0), (M4, 1)]
-    if keys is not None:
-        lists[0], lists[1], units = ([base[string.ascii_letters.index(ch)] for ch in key] for base, key in zip(lists[:2] + [units], keys))
+ORDER = (
+    "acbdgihjEuyFHGmInJosAptvzBekflqwrxCKDLM",
+    "adjmbecfknlosutvzBACGIHJghipqrwxyDKELFM",
+    "bagflqpyvudinskxtmchACrejowBEDz",
+)
+
+
+def make_lists(plan):
+    it, un = plan
+    base = [[n for n in it if it[n][0] == k] for k in range(len(ORDER) - 1)] + [list(un)]
+    *lists, units = ([names[string.ascii_letters.index(ch)] for ch in key] for names, key in zip(base, ORDER))
     return lists, units
 
-
-ORDER = (
-    "tafcewhbgpdlvixnjyrkqmsozAuBCDEGIFHKJLM",
-    "abdcejfrhglimknopqtsuvwxyBzACDEFGHKJIML",
-    "BmhownAsbpEjrlayvqDkcxdtgfCziue",
-)
 
 RATE = (22.5, 22.5, 1.7, 0.4)
 DELAY = (3.0, 3.0, 1.5, 1.5)
@@ -143,8 +131,8 @@
     pend, now, order, panels, waits = list(units), 0.0, [], [], []
     late = [n for n in it if it[n][0] >= 2]
     rank = {u: i for i, u in enumerate(units)}
-    user = lambda n: (PANEL_OF[n[0]], n[1] // 2 if n[0] == L4 else n[1])
-    panel_rank = lambda n: rank[user(n)] if n[0] in PANEL_OF else -1
+    user = lambda n: (PANEL_OF[n[0]], PART_OF[n[1]] if n[0] in (L4, L5) else n[1])
+    panel_rank = lambda n: rank[user(n)] if n[0] in PANEL_OF else rank[{LX: M4, LH: M5}[n[0]], 0] if n[0] in (LX, LH) else -1
     gone = set()
     big = 1e9
 
@@ -231,7 +219,7 @@
             self.left(name)
 
 
-N_REMOTE = 196
+N_REMOTE = 208
 N_LOCAL = 80
 
 
@@ -318,8 +306,10 @@
             return [(XF.at[0, group(r)[0], span(r)], XPB.at[group(r)[0], span(r)], "P")]
         if kind == HP:
             return [(hbuf.at[group(r)[0], span(r)], HPB.at[group(r)[0], span(r)], "P")]
-        if kind == CP:
-            return [(DF.at[:, group(r)[0], span(r), theirs], DPB.at[:, group(r)[0], span(r)], "P")]
+        if kind in (CP, CF):
+            b = group(r)[0]
+            js = (pl.ds(0, 2), pl.ds(3, 1)) if kind == CP else (pl.ds(2, 1),)
+            return [(DF.at[j, b, span(r), theirs], DPB.at[j, b, span(r)], "P") for j in js]
         if kind == CS:
             b, _, n = group(r)
             s = dct.at[r % 2, pl.ds(0, RING * n)]
@@ -343,7 +333,7 @@
             m = {L1: XF, L2: GF, L3: DF}[kind]
             return [(m.at[:, b, span(r)], pan.at[slot_of[name], :, pl.ds(0, RING * n)], None)]
         if kind in (L5, L4):
-            m, p, j = (GF, GPB, O5[r]) if kind == L5 else (DF, DPB, r)
+            m, p, j = (GF, GPB, O5[r]) if kind == L5 else (DF, DPB, O4[r])
             s = pan.at[slot_of[name]]
             return [(m.at[j, :, :, mine], s.at[:, :, lo], None), (p.at[j], s.at[:, :, hi], None)]
         if kind == LH:
@@ -413,26 +403,24 @@
             def body(t):
                 f[t, rows, :] = total([(p[j, rows, :], wun[2 * j + t], NT) for j in range(RING)])
             loop(2, body)
-        elif kind == M5:
-            p = pan.at[slot_of[L5, r]]
-
-            def body(t):
-                ms = pl.ds(pl.multiple_of(t * dh, dh), dh)
-                s = total([(hbuf[g, :, ms], p[g, :, lo], TN) for g in range(NB)] + [(wds[g, :, ms], p[g, :, hi], TN) for g in range(NB)])
-                obuf[r, t] = s.astype(jnp.bfloat16)
-            loop(2, body)
-            if O5[r] == 0:
-                cp.add((OUT, kind, r), [(obuf.at[r], dwd.at[:, x], None)])
-        elif kind == M4:
-            s0, s1 = slot_of[L4, 2 * r], slot_of[L4, 2 * r + 1]
+        elif kind in (M5, M4):
+            i0, m = PARTS[r]
+            s0, s1 = (slot_of[L5 if kind == M5 else L4, i] for i in (i0, i0 + m - 1))
+            j0, j1 = ((O5 if kind == M5 else O4)[i] for i in (i0, i0 + m - 1))
+            own, par, p0 = (hbuf, wds, 0) if kind == M5 else (wus, wus, NB)
 
             def body(i):
-                e, t = i // 2, lax.rem(i, 2)
+                e, t = (0, i) if m == 1 else (i // 2, lax.rem(i, 2))
                 p = pan.at[s0 + e * (s1 - s0)]
                 ms = pl.ds(pl.multiple_of(t * dh, dh), dh)
-                s = total([(wus[g, :, ms], p[g, :, lo], TN) for g in range(NB)] + [(wus[NB + g, :, ms], p[g, :, hi], TN) for g in range(NB)])
-                dwu[t, :, cols(2 * r + e)] = s.astype(jnp.bfloat16)
-            loop(4, body)
+                s = total([(own[g, :, ms], p[g, :, lo], TN) for g in range(NB)] + [(par[p0 + g, :, ms], p[g, :, hi], TN) for g in range(NB)])
+                if kind == M5:
+                    obuf[i0 + e, t] = s.astype(jnp.bfloat16)
+                else:
+                    dwu[t, :, cols(j0 + e * (j1 - j0))] = s.astype(jnp.bfloat16)
+            loop(2 * m, body)
+            if kind == M5 and O5[i0] == 0:
+                cp.add((OUT, kind), [(obuf.at[i0], dwd.at[:, x], None)])
         else:
             b, first, n = group(r)
             f = ft.at[r % 2]
@@ -477,7 +465,7 @@
     up_out = P(("dp", "cy"), ("cz", "cx"))
     down_out = P(("dp", "cz"), ("cy", "cx"))
     plan = make_plan()
-    order, panels, _, _ = make_order(plan, *make_lists(ORDER))
+    order, panels, _, _ = make_order(plan, *make_lists(plan))
 
     def local_step(x_act, w_up, w_down, z_grad):
         t_loc, d_loc = x_act.shape

time: 365 us -> 361 us (0.989)
  Pallas kernels: 357 us -> 352 us
    pallas_call x1, Pallas kernels: 357 us -> 352 us  [local_step(): pl.pallas_call(functools.partial(kernel, plan, order, panels), out_shape=...]
where the time goes in v4:
time: 361 us; the launch traced here: 359 us
  Pallas kernels  352 us (98%)
  local copies, waits for them, and re-layouts  6.69 us (2%)
    pallas_call x1, Pallas kernels, local_step(): pl.pallas_call(functools.partial(kernel, plan, order, panels), out_shape=...  352 us

profile of v4, /device:TPU:96, one launch (start us, length us, event | category | flops | bytes accessed | tf_op | source)
XLA Modules:
  0.0 359.1 jit_solution(3079113333805459152)
XLA Ops:
  0.6 351.7 %mlp_bwd.1 = (bf16[4,128,1024]{2,1,0:T(8,128)(2,1)S(1)}, bf16[2,512,2048]{2,1,0:T(8,128)(2,1)S(1)}, bf16[2,4,512,512]{3,2,1,0:T(8,128)(2,1)}, bf16[4,4,512,1024]...) custom-call(bf16[4,128,1024]{2,1,0:T(8,128)(2,1)} %bitcast.12, ...), custom_call_target="tpu_custom_call" | custom-call | tf_op jit(solution)/shard_map/mlp_bwd/pallas_call | solution.py:496
  352.4 1.0 copy.10
  353.3 0.0 copy-start
  353.3 2.1 copy.11
  355.5 1.6 copy-done
  357.0 2.0 copy.12
Async XLA Ops:
  353.3 3.7 %copy-start = (bf16[2,4,512,512]{3,2,1,0:T(8,128)(2,1)S(1)}, bf16[2,4,512,512]{3,2,1,0:T(8,128)(2,1)}, u32[]{:S(2)}) copy-start(bf16[2,4,512,512]{3,2,1,0:T(8,128)(2,1)} %get-tuple-element.8) | copy-start | bytes 12582916

commit v5 on v4

--- a/solution.py
+++ b/solution.py
@@ -145,7 +145,7 @@
         waits.append((k, start - free[k], n))
         free[k] = start + it[n][1] * RATE[k]
         done[n] = free[k] + DELAY[k]
-        order.append(n)
+        order.append((n, now))
 
     while True:
         for k in (0, 1):
@@ -162,7 +162,7 @@
         can = [u for u in pend if all(done.get(d, big) <= now for d in un[u][1])]
         if can:
             pend.remove(can[0])
-            order.append(can[0])
+            order.append((can[0], now))
             now += un[can[0]][0]
             done[can[0]] = now
             gone.add(can[0])
@@ -172,46 +172,64 @@
             break
         now = min(later)
     assert not pend and not late and all(pos[k] == len(lists[k]) for k in (0, 1)), (pend, late, pos)
-    return order, panels, max(done.values()), waits
+    return [(n, [m for m in it if t - 30 < done[m] <= t - 2 and it[m][0] < 3]) for n, t in order], panels, max(done.values()), waits
 
 
 class Copies:
+    BACK = {"R": "L", "L": "R", "U": "N", "N": "U", "P": "P"}
+
     def __init__(self, send, recv, local, peers):
         self.send, self.recv, self.local, self.peers = send, recv, local, peers
-        self.n_remote = self.n_local = 0
-        self.by_name = {}
+        self.by_name, self.clock = {}, 0
+        self.used = {"send": 0, "recv": 0, "local": 0}
+        self.free = {"send": [], "local": []} | {to: [] for to in peers}
+        self.waited = {to: [] for to in peers}
+
+    def take(self, kind, pool):
+        if self.free[pool]:
+            return self.free[pool].pop()
+        self.used[kind] += 1
+        return self.used[kind] - 1
 
     def add(self, name, pairs):
         made = []
         for src, dst, to in pairs:
+            self.clock += 1
             if to is None:
-                c = pltpu.make_async_copy(src, dst, self.local.at[self.n_local])
-                self.n_local += 1
+                i = self.take("local", "local")
+                made.append([pltpu.make_async_copy(src, dst, self.local.at[i]), to, self.clock, i, None])
             else:
                 axis, idx = self.peers[to]
-                c = pltpu.make_async_remote_copy(
-                    src, dst, self.send.at[self.n_remote], self.recv.at[self.n_remote],
-                    device_id={axis: idx}, device_id_type=MESH)
-                self.n_remote += 1
-            made.append([c, to, False, False])
-            c.start()
+                i, j = self.take("send", "send"), self.take("recv", to)
+                c = pltpu.make_async_remote_copy(src, dst, self.send.at[i], self.recv.at[j], device_id={axis: idx}, device_id_type=MESH)
+                made.append([c, to, self.clock, i, j])
+            made[-1][0].start()
         self.by_name.setdefault(name, []).extend(made)
 
     def arrived(self, name):
         for m in self.by_name.get(name, ()):
-            if not m[2]:
-                m[2] = True
-                m[0].wait() if m[1] is None else m[0].wait_recv()
+            c, to, started, i, j = m
+            self.clock += 1
+            if to is None and i is not None:
+                c.wait()
+                self.free["local"].append(i)
+                m[3] = None
+            elif j is not None:
+                c.wait_recv()
+                self.waited[to].append((self.clock, j))
+                m[4] = None
+                back = self.BACK[to]
+                self.free[back] += [k for t, k in self.waited[back] if t < started]
+                self.waited[back] = [(t, k) for t, k in self.waited[back] if t >= started]
 
     def left(self, name):
         for m in self.by_name.get(name, ()):
             if m[1] is None:
-                if not m[2]:
-                    m[2] = True
-                    m[0].wait()
-            elif not m[3]:
-                m[3] = True
+                self.arrived(name)
+            elif m[3] is not None:
                 m[0].wait_send()
+                self.free["send"].append(m[3])
+                m[3] = None
 
     def finish(self):
         for name in list(self.by_name):
@@ -219,8 +237,7 @@
             self.left(name)
 
 
-N_REMOTE = 208
-N_LOCAL = 80
+N_SEND, N_RECV, N_LOCAL = 20, 79, 16
 
 
 def kernel(plan, order, panels, xa, wu, wd, za, dx, dwu, dwd, XF, GF, DF, GPB, DPB, XPB, HPB, su, sd, sw,
@@ -433,7 +450,9 @@
                 for h in range(2):
                     dx[b, rs, h * dh:(h + 1) * dh] = (f[h, own(0), :] + rrc[b, 0, h, rs, :] + rrc[b, 1, h, rs, :]).astype(jnp.bfloat16)
 
-    for name in order:
+    for name, gone in order:
+        for d in gone:
+            cp.left(d)
         for d in (it[name][2] if name in it else un[name][1]):
             cp.arrived(d)
         if name[0] == OWN:
@@ -454,7 +473,7 @@
         else:
             unit(name)
     cp.finish()
-    assert cp.n_remote <= N_REMOTE and cp.n_local <= N_LOCAL, (cp.n_remote, cp.n_local)
+    assert tuple(cp.used.values()) == (N_SEND, N_RECV, N_LOCAL), cp.used
 
 
 def solution(mesh):
@@ -490,7 +509,7 @@
             pltpu.VMEM((NB, 2, rows, dh), f32), pltpu.VMEM((NB, 2, 2, rows, dh), f32),
             pltpu.VMEM((RING, CORES, sub, dh), bf),
             pltpu.VMEM((grp, sub), f32),
-            pltpu.SemaphoreType.DMA((N_REMOTE,)), pltpu.SemaphoreType.DMA((N_REMOTE,)), pltpu.SemaphoreType.DMA((N_LOCAL,)),
+            pltpu.SemaphoreType.DMA((N_SEND,)), pltpu.SemaphoreType.DMA((N_RECV,)), pltpu.SemaphoreType.DMA((N_LOCAL,)),
         ]
         any_spec = pl.BlockSpec(memory_space=pl.ANY)
         res = pl.pallas_call(

time: 361 us -> 357 us (0.989)
  Pallas kernels: 352 us -> 348 us
    pallas_call x1, Pallas kernels: 352 us -> 348 us  [local_step(): pl.pallas_call(functools.partial(kernel, plan, order, panels), out_shape=...]
where the time goes in v5:
time: 357 us; the launch traced here: 355 us
  Pallas kernels  348 us (97%)
  local copies, waits for them, and re-layouts  6.69 us (2%)
    pallas_call x1, Pallas kernels, local_step(): pl.pallas_call(functools.partial(kernel, plan, order, panels), out_shape=...  348 us

profile of v5, /device:TPU:96, one launch (start us, length us, event | category | flops | bytes accessed | tf_op | source)
XLA Modules:
  0.0 355.4 jit_solution(11262899040479330856)
XLA Ops:
  0.6 348.1 %mlp_bwd.1 = (bf16[4,128,1024]{2,1,0:T(8,128)(2,1)S(1)}, bf16[2,512,2048]{2,1,0:T(8,128)(2,1)S(1)}, bf16[2,4,512,512]{3,2,1,0:T(8,128)(2,1)}, bf16[4,4,512,1024]...) custom-call(bf16[4,128,1024]{2,1,0:T(8,128)(2,1)} %bitcast.12, ...), custom_call_target="tpu_custom_call" | custom-call | tf_op jit(solution)/shard_map/mlp_bwd/pallas_call | solution.py:515
  348.7 1.0 copy.10
  349.7 0.0 copy-start
  349.7 2.1 copy.11
  351.8 1.6 copy-done
  353.4 2.0 copy.12
Async XLA Ops:
  349.7 3.7 %copy-start = (bf16[2,4,512,512]{3,2,1,0:T(8,128)(2,1)S(1)}, bf16[2,4,512,512]{3,2,1,0:T(8,128)(2,1)}, u32[]{:S(2)}) copy-start(bf16[2,4,512,512]{3,2,1,0:T(8,128)(2,1)} %get-tuple-element.8) | copy-start | bytes 12582916

commit v6 on v5

--- a/solution.py
+++ b/solution.py
@@ -34,7 +34,7 @@
 
 
 (XS, XR, W2, W1, WR, CS, CR, O2, O1, OR, YA, YB, YF, YR, Q2, QD, QS, WN, WP, GP, XP, HP, CP, CF,
- OWN, L1, L2, L3, L4, L5, LX, LH, M1, M2, M3, M4, M5, QA, QF, OUT) = range(40)
+ ST, OWN, L1, L2, L3, L4, L5, LX, LH, M1, M2, M3, M4, M5, QA, QF, OUT) = range(41)
 PANEL_OF = {L1: M1, L2: M2, L3: M3, L4: M4, L5: M5}
 O5 = (2, 1, 3, 0)
 O4 = (0, 1, 3, 2)
@@ -44,6 +44,10 @@
 
 def full(a, r):
     return [(XS, a, r), (XR, a, r), (YR, a, r), (OWN,)] + ([(YA, a, r), (YB, a, r)] if r < EARLY else [(YF, a, r)])
+
+
+def staged(r):
+    return GROUPS[r][2] == 8
 
 
 def make_plan():
@@ -66,10 +70,11 @@
         it[GP, r] = (2, 8 * q, full(G, r))
         it[XP, r] = (2, 4 * q, full(X, r))
         it[HP, r] = (2, 4 * q, [(M2, r)])
-        it[CS, r] = (0, 4 * q, [(M2, r)])
+        it[ST, r] = (3, f, [(M2, r)])
+        it[CS, r] = (0, f, [(ST, r) if staged(r) else (M2, r)])
         it[CR, r] = (0, 2 * q, [(CS, r)])
-        dc = [(CS, r), (CR, r)]
-        it[CP, r] = (2, 6 * q, [(CS, r)])
+        dc = [(ST, r), (CS, r), (CR, r)]
+        it[CP, r] = (2, 6 * q, [(ST, r), (CS, r)])
         it[CF, r] = (2, 2 * q, [(CR, r)])
         it[Q2, r] = (1, q, [(M3, r)])
         it[QD, r] = (1, q, [(M3, r)])
@@ -98,7 +103,7 @@
     it[(OR,)] = (0, 0.5, [(O2,)])
     for p in range(RING):
         it[L5, p] = (3, 4, [(GP, r) for r in groups] + sum([full(G, r) for r in groups], []))
-        it[L4, p] = (3, 4, [(CF if O4[p] == 2 else CP, r) for r in groups] + [(CR if O4[p] == 2 else CS, r) for r in groups])
+        it[L4, p] = (3, 4, [(CF if O4[p] == 2 else CP, r) for r in groups] + [((ST, CS, CS, CR)[p], r) for r in groups])
     it[(LH,)] = (3, 4, [(HP, r) for r in groups] + [(M2, r) for r in groups])
     it[(LX,)] = (3, 8, [(XP, r) for r in groups] + [(M5, 0)])
     for p, (first, n) in enumerate(PARTS):
@@ -108,9 +113,9 @@
 
 
 ORDER = (
-    "acbdgihjEuyFHGmInJosAptvzBekflqwrxCKDLM",
-    "adjmbecfknlosutvzBACGIHJghipqrwxyDKELFM",
-    "bagflqpyvudinskxtmchACrejowBEDz",
+    "acbdgimInhjEFHGuyJosAptvzBekflqwrxCKDLM",
+    "adjbecmknfoslutvzBACGIHJghipqrwxyDKELFM",
+    "shympwukqjnlfAogBaivCetxDbrzdcE",
 )
 
 
@@ -237,11 +242,11 @@
             self.left(name)
 
 
-N_SEND, N_RECV, N_LOCAL = 20, 79, 16
+N_SEND, N_RECV, N_LOCAL = 24, 77, 16
 
 
 def kernel(plan, order, panels, xa, wu, wd, za, dx, dwu, dwd, XF, GF, DF, GPB, DPB, XPB, HPB, su, sd, sw,
-           wus, wds, wun, hbuf, pan, ft, dct, rst, rrc, obuf, acc, send, recv, local):
+           wus, wds, wun, hbuf, pan, ft, rst, rrc, obuf, acc, send, recv, local):
     it, un = plan
     x, y, c = lax.axis_index("cy"), lax.axis_index("cz"), lax.axis_index("cx")
     peers = {
@@ -326,15 +331,18 @@
         if kind in (CP, CF):
             b = group(r)[0]
             js = (pl.ds(0, 2), pl.ds(3, 1)) if kind == CP else (pl.ds(2, 1),)
-            return [(DF.at[j, b, span(r), theirs], DPB.at[j, b, span(r)], "P") for j in js]
+            return [(DF.at[j, b, 1 - c, span(r)], DPB.at[j, b, span(r)], "P") for j in js]
+        if kind == ST:
+            b = group(r)[0]
+            return [(obuf.at[2, :, span(r)], DF.at[0, b, :, span(r)], None)]
         if kind == CS:
-            b, _, n = group(r)
-            s = dct.at[r % 2, pl.ds(0, RING * n)]
-            return both((s, DF.at[3, b, span(r)]), (s, DF.at[1, b, span(r)])) + [(s, DF.at[0, b, span(r)], None)]
+            b = group(r)[0]
+            m = DF.at[0, b, :, span(r)] if staged(r) else obuf.at[2, :, span(r)]
+            return both((m, DF.at[3, b, :, span(r)]), (m, DF.at[1, b, :, span(r)]))
         if kind == CR:
             b, first, n = group(r)
             f, s = (pl.ds(RING * first + h * 2 * n, 2 * n) for h in range(2))
-            return both((DF.at[3, b, f], DF.at[2, b, f]), (DF.at[1, b, s], DF.at[2, b, s]))
+            return both((DF.at[3, b, :, f], DF.at[2, b, :, f]), (DF.at[1, b, :, s], DF.at[2, b, :, s]))
         if kind in (Q2, QD, QS):
             b, first, n = group(r)
             f = ft.at[r % 2]
@@ -347,12 +355,14 @@
             return updn((f.at[0, own(1)], rrc.at[b, 0, 0, rs]), (f.at[1, own(3)], rrc.at[b, 1, 1, rs]))
         if kind in (L1, L2, L3):
             b, _, n = group(r)
-            m = {L1: XF, L2: GF, L3: DF}[kind]
-            return [(m.at[:, b, span(r)], pan.at[slot_of[name], :, pl.ds(0, RING * n)], None)]
+            to = pan.at[slot_of[name], :, pl.ds(0, RING * n)]
+            if kind == L3:
+                return [(DF.at[:, b, h, span(r)], to.at[:, :, h * sub:(h + 1) * sub], None) for h in range(CORES)]
+            return [((XF if kind == L1 else GF).at[:, b, span(r)], to, None)]
         if kind in (L5, L4):
-            m, p, j = (GF, GPB, O5[r]) if kind == L5 else (DF, DPB, O4[r])
+            m, p = (GF.at[O5[r], :, :, mine], GPB.at[O5[r]]) if kind == L5 else (DF.at[O4[r], :, c], DPB.at[O4[r]])
             s = pan.at[slot_of[name]]
-            return [(m.at[j, :, :, mine], s.at[:, :, lo], None), (p.at[j], s.at[:, :, hi], None)]
+            return [(m, s.at[:, :, lo], None), (p, s.at[:, :, hi], None)]
         if kind == LH:
             return [(HPB, wds.at[0:4], None)]
         if kind == LX:
@@ -393,9 +403,8 @@
             loop(2, body)
         elif kind == M2:
             p = pan.at[slot_of[L2, r]]
-            if r >= 2:
-                cp.left((CS, r - 2))
-            d = dct.at[r % 2]
+            if r > 0 and staged(r - 1):
+                cp.arrived((ST, r - 1))
             step = min(32, RING * n)
 
             def body(t):
@@ -407,7 +416,7 @@
                     hs = pl.ds(pl.multiple_of(RING * first + e * step, step), step)
                     g, s = gelu_parts(hbuf[b, hs, ns].astype(jnp.float32))
                     hbuf[b, hs, ns] = g.astype(jnp.bfloat16)
-                    d[rs, ns] = (acc[rs, :] * s).astype(jnp.bfloat16)
+                    obuf[2, t, hs, :] = (acc[rs, :] * s).astype(jnp.bfloat16)
                 loop(RING * n // step, elem)
             loop(2, body)
         elif kind == M3:
@@ -425,19 +434,23 @@
             s0, s1 = (slot_of[L5 if kind == M5 else L4, i] for i in (i0, i0 + m - 1))
             j0, j1 = ((O5 if kind == M5 else O4)[i] for i in (i0, i0 + m - 1))
             own, par, p0 = (hbuf, wds, 0) if kind == M5 else (wus, wus, NB)
+            if kind == M5 and i0 + m - 1 == 2:
+                for g in range(NG):
+                    cp.arrived((ST, g))
+                    cp.left((CS, g))
 
             def body(i):
                 e, t = (0, i) if m == 1 else (i // 2, lax.rem(i, 2))
                 p = pan.at[s0 + e * (s1 - s0)]
                 ms = pl.ds(pl.multiple_of(t * dh, dh), dh)
                 s = total([(own[g, :, ms], p[g, :, lo], TN) for g in range(NB)] + [(par[p0 + g, :, ms], p[g, :, hi], TN) for g in range(NB)])
-                if kind == M5:
+                if kind == M5 and O5[i0] == 0:
+                    dwd[t, x] = s.astype(jnp.bfloat16)
+                elif kind == M5:
                     obuf[i0 + e, t] = s.astype(jnp.bfloat16)
                 else:
                     dwu[t, :, cols(j0 + e * (j1 - j0))] = s.astype(jnp.bfloat16)
             loop(2 * m, body)
-            if kind == M5 and O5[i0] == 0:
-                cp.add((OUT, kind), [(obuf.at[i0], dwd.at[:, x], None)])
         else:
             b, first, n = group(r)
             f = ft.at[r % 2]
@@ -497,17 +510,17 @@
         wd = w_down.reshape(CORES, RING, sub, dh)
         hbm = lambda *s: jax.ShapeDtypeStruct(s, bf)
         outs = (
-            pltpu.VMEM((NB, rows, d_loc), bf), pltpu.VMEM((2, dh, f_loc), bf), hbm(CORES, RING, sub, dh),
-            hbm(RING, NB, grp, d_loc), hbm(RING, NB, grp, d_loc), hbm(RING, NB, grp, 2 * sub),
+            pltpu.VMEM((NB, rows, d_loc), bf), pltpu.VMEM((2, dh, f_loc), bf), pltpu.VMEM((CORES, RING, sub, dh), bf),
+            hbm(RING, NB, grp, d_loc), hbm(RING, NB, grp, d_loc), hbm(RING, NB, CORES, grp, sub),
             hbm(RING, NB, grp, sub), hbm(RING, NB, grp, sub), hbm(NB, grp, d_loc), hbm(NB, grp, 2 * sub),
             hbm(2, dh, sub), hbm(2, sub, dh), hbm(2, sub, dh),
         )
         scratch = [
             pltpu.VMEM((2 * RING, dh, 2 * sub), bf), pltpu.VMEM((2 * RING, sub, d_loc), bf), pltpu.VMEM((2 * RING, dh, 2 * sub), bf),
             pltpu.VMEM((NB, grp, 2 * sub), bf), pltpu.VMEM((PAN, RING, grp, d_loc), bf),
-            pltpu.VMEM((2, 2, grp, dh), f32), pltpu.VMEM((2, grp, 2 * sub), bf),
+            pltpu.VMEM((2, 2, grp, dh), f32),
             pltpu.VMEM((NB, 2, rows, dh), f32), pltpu.VMEM((NB, 2, 2, rows, dh), f32),
-            pltpu.VMEM((RING, CORES, sub, dh), bf),
+            pltpu.VMEM((3, CORES, sub, dh), bf),
             pltpu.VMEM((grp, sub), f32),
             pltpu.SemaphoreType.DMA((N_SEND,)), pltpu.SemaphoreType.DMA((N_RECV,)), pltpu.SemaphoreType.DMA((N_LOCAL,)),
         ]
@@ -516,9 +529,9 @@
             functools.partial(kernel, plan, order, panels),
             out_shape=outs,
             in_specs=[any_spec] * 4,
-            out_specs=[pl.BlockSpec(memory_space=pltpu.VMEM)] * 2 + [any_spec] * (len(outs) - 2),
+            out_specs=[pl.BlockSpec(memory_space=pltpu.VMEM)] * 3 + [any_spec] * (len(outs) - 3),
             scratch_shapes=scratch,
-            compiler_params=pltpu.CompilerParams(collective_id=0, has_side_effects=True, vmem_limit_bytes=61800000),
+            compiler_params=pltpu.CompilerParams(collective_id=0, has_side_effects=True, vmem_limit_bytes=57600000),
             name="mlp_bwd",
         )(xa, wu, wd, za)
         return (res[0].reshape(t_loc, d_loc), res[1].reshape(w_up.shape), res[2].reshape(w_down.shape))

time: 357 us -> 354 us (level)
  no operation moved by 1% of the time
where the time goes in v6:
time: 354 us; the launch traced here: 353 us
  Pallas kernels  348 us (98%)
  local copies, waits for them, and re-layouts  5 us (1%)
    pallas_call x1, Pallas kernels, local_step(): pl.pallas_call(functools.partial(kernel, plan, order, panels), out_shape=...  348 us

profile of v6, /device:TPU:96, one launch (start us, length us, event | category | flops | bytes accessed | tf_op | source)
XLA Modules:
  0.0 353.2 jit_solution(6212398117563444716)
XLA Ops:
  0.6 347.5 %mlp_bwd.1 = (bf16[4,128,1024]{2,1,0:T(8,128)(2,1)S(1)}, bf16[2,512,2048]{2,1,0:T(8,128)(2,1)S(1)}, bf16[2,4,512,512]{3,2,1,0:T(8,128)(2,1)S(1)}, bf16[4,4,512,1...) custom-call(bf16[4,128,1024]{2,1,0:T(8,128)(2,1)} %bitcast.12, ...), custom_call_target="tpu_custom_call" | custom-call | tf_op jit(solution)/shard_map/mlp_bwd/pallas_call | solution.py:528
  348.2 1.0 copy.10
  349.1 2.0 copy.11
  351.1 2.0 copy.12

commit v7 on v6

--- a/solution.py
+++ b/solution.py
@@ -39,7 +39,7 @@
 O5 = (2, 1, 3, 0)
 O4 = (0, 1, 3, 2)
 PARTS = ((0, 1), (1, 2), (3, 1))
-PART_OF = (0, 1, 1, 2)
+PART_OF = [p for p, (_, n) in enumerate(PARTS) for _ in range(n)]
 
 
 def full(a, r):
@@ -113,9 +113,9 @@
 
 
 ORDER = (
-    "acbdgimInhjEFHGuyJosAptvzBekflqwrxCKDLM",
-    "adjbecmknfoslutvzBACGIHJghipqrwxyDKELFM",
-    "shympwukqjnlfAogBaivCetxDbrzdcE",
+    "acbdimgInhjEHGFyJosuApzteBvkflqwrxCKDML",
+    "admjbecsknfolutvzBACGIHJghipqrwxyDKELFM",
+    "yompqhsjlwunkfAgBtxCiveabzcrEDd",
 )
 
 
@@ -126,13 +126,14 @@
     return lists, units
 
 
-RATE = (22.5, 22.5, 1.7, 0.4)
-DELAY = (3.0, 3.0, 1.5, 1.5)
+LINKS = range(4)
+RATE = (22.5,) * 2 + (1.7, 0.4)
+DELAY = (3.0,) * 2 + (1.5,) * 2
 
 
 def make_order(plan, lists, units):
     it, un = plan
-    done, free, pos = {}, [0.0] * 4, [0] * 4
+    done, free, pos = {}, [0.0 for _ in LINKS], [0 for _ in LINKS]
     pend, now, order, panels, waits = list(units), 0.0, [], [], []
     late = [n for n in it if it[n][0] >= 2]
     rank = {u: i for i, u in enumerate(units)}
@@ -242,7 +243,7 @@
             self.left(name)
 
 
-N_SEND, N_RECV, N_LOCAL = 24, 77, 16
+N_SEND, N_RECV, N_LOCAL = 26, 79, 16
 
 
 def kernel(plan, order, panels, xa, wu, wd, za, dx, dwu, dwd, XF, GF, DF, GPB, DPB, XPB, HPB, su, sd, sw,
@@ -489,6 +490,15 @@
     assert tuple(cp.used.values()) == (N_SEND, N_RECV, N_LOCAL), cp.used
 
 
+def write_out(dx, dwu, dwd, dx_out, dwu_out, dwd_out, sem):
+    pairs = [(a.at[i], b.at[i]) for a, b in ((dx, dx_out), (dwu, dwu_out), (dwd, dwd_out)) for i in range(a.shape[0])]
+    copies = [pltpu.make_async_copy(a, b, sem.at[i]) for i, (a, b) in enumerate(pairs)]
+    for copy in copies:
+        copy.start()
+    for copy in copies:
+        copy.wait()
+
+
 def solution(mesh):
     assert mesh.shape["cy"] == RING and mesh.shape["cz"] == RING and mesh.shape["cx"] == CORES
     row_spec = P(("dp", "cx", "cz"), "cy")
@@ -534,6 +544,16 @@
             compiler_params=pltpu.CompilerParams(collective_id=0, has_side_effects=True, vmem_limit_bytes=57600000),
             name="mlp_bwd",
         )(xa, wu, wd, za)
-        return (res[0].reshape(t_loc, d_loc), res[1].reshape(w_up.shape), res[2].reshape(w_down.shape))
+        outs = [pltpu.with_memory_space_constraint(o, pltpu.VMEM) for o in res[:3]]
+        outs = pl.pallas_call(
+            write_out,
+            out_shape=[jax.ShapeDtypeStruct(o.shape, bf) for o in outs],
+            in_specs=[pl.BlockSpec(memory_space=pltpu.VMEM) for _ in outs],
+            out_specs=[any_spec for _ in outs],
+            scratch_shapes=[pltpu.SemaphoreType.DMA((sum(o.shape[0] for o in outs),))],
+            compiler_params=pltpu.CompilerParams(vmem_limit_bytes=1 << 20),
+            name="write_out",
+        )(*outs)
+        return tuple(o.reshape(a.shape) for o, a in zip(outs, (x_act, w_up, w_down)))
 
     return jax.shard_map(local_step, mesh=mesh, in_specs=(row_spec, up_spec, down_spec, row_spec), out_specs=(row_spec, up_out, down_out), check_vma=False)

time: 354 us -> 352 us (level)
  local copies, waits for them, and re-layouts: 5 us -> 0 us
    unnamed x3 -> x0, local copies, waits for them, and re-layouts: 5 us -> none
    pallas_call x0 -> x1, Pallas kernels: none -> 3.75 us  [local_step(): pl.pallas_call(write_out, out_shape=[jax.ShapeDtypeStruct(o.shape, bf) fo...]
where the time goes in v7:
time: 352 us
  Pallas kernels  351 us (100%)
    pallas_call x1, Pallas kernels, local_step(): pl.pallas_call(functools.partial(kernel, plan, order, panels), out_shape=...  347 us

profile of v7, /device:TPU:96, one launch (start us, length us, event | category | flops | bytes accessed | tf_op | source)
XLA Modules:
  0.0 352.0 jit_solution(7013202022693201321)
XLA Ops:
  0.6 347.4 %mlp_bwd.1 = (bf16[4,128,1024]{2,1,0:T(8,128)(2,1)S(1)}, bf16[2,512,2048]{2,1,0:T(8,128)(2,1)S(1)}, bf16[2,4,512,512]{3,2,1,0:T(8,128)(2,1)S(1)}, bf16[4,4,512,1...) custom-call(bf16[4,128,1024]{2,1,0:T(8,128)(2,1)} %bitcast.9, ...), custom_call_target="tpu_custom_call" | custom-call | tf_op jit(solution)/shard_map/mlp_bwd/pallas_call | solution.py:538
  348.1 3.7 %write_out.1 = (bf16[4,128,1024]{2,1,0:T(8,128)(2,1)}, bf16[2,512,2048]{2,1,0:T(8,128)(2,1)}, bf16[2,4,512,512]{3,2,1,0:T(8,128)(2,1)}) custom-call(bf16[4,128,1024]{2,1,0:T(8,128)(2,1)S(1)} %get-tuple-element.9.dx, bf16[2,512,2048]{2,1,0:T(8,128)(2,1)S(1)} %get-tuple-element.10.dwu, bf16[2,4,512,512]{3,2,1,0:T(8,128)(2,1)S(1)} %get-tuple-element.11.dwd), custom_call_target="tpu_custom_call" | custom-call | tf_op jit(solution)/shard_map/write_out/pallas_call | solution.py:548

commit v8 on v7

--- a/solution.py
+++ b/solution.py
@@ -243,7 +243,7 @@
             self.left(name)
 
 
-N_SEND, N_RECV, N_LOCAL = 26, 79, 16
+N_SEND, N_RECV, N_LOCAL = 26, 54, 16
 
 
 def kernel(plan, order, panels, xa, wu, wd, za, dx, dwu, dwd, XF, GF, DF, GPB, DPB, XPB, HPB, su, sd, sw,
@@ -466,6 +466,7 @@
 
     for name, gone in order:
         for d in gone:
+            cp.arrived(d)
             cp.left(d)
         for d in (it[name][2] if name in it else un[name][1]):
             cp.arrived(d)

time: 352 us -> 352 us (level)
  no operation moved by 1% of the time
where the time goes in v8:
time: 352 us
  Pallas kernels  351 us (100%)
    pallas_call x1, Pallas kernels, local_step(): pl.pallas_call(functools.partial(kernel, plan, order, panels), out_shape=...  347 us

profile of v8, /device:TPU:96, one launch (start us, length us, event | category | flops | bytes accessed | tf_op | source)
XLA Modules:
  0.0 351.8 jit_solution(6970903944411917590)
XLA Ops:
  0.6 347.2 %mlp_bwd.1 = (bf16[4,128,1024]{2,1,0:T(8,128)(2,1)S(1)}, bf16[2,512,2048]{2,1,0:T(8,128)(2,1)S(1)}, bf16[2,4,512,512]{3,2,1,0:T(8,128)(2,1)S(1)}, bf16[4,4,512,1...) custom-call(bf16[4,128,1024]{2,1,0:T(8,128)(2,1)} %bitcast.9, ...), custom_call_target="tpu_custom_call" | custom-call | tf_op jit(solution)/shard_map/mlp_bwd/pallas_call | solution.py:539
  347.8 3.7 %write_out.1 = (bf16[4,128,1024]{2,1,0:T(8,128)(2,1)}, bf16[2,512,2048]{2,1,0:T(8,128)(2,1)}, bf16[2,4,512,512]{3,2,1,0:T(8,128)(2,1)}) custom-call(bf16[4,128,1024]{2,1,0:T(8,128)(2,1)S(1)} %get-tuple-element.9.dx, bf16[2,512,2048]{2,1,0:T(8,128)(2,1)S(1)} %get-tuple-element.10.dwu, bf16[2,4,512,512]{3,2,1,0:T(8,128)(2,1)S(1)} %get-tuple-element.11.dwd), custom_call_target="tpu_custom_call" | custom-call | tf_op jit(solution)/shard_map/write_out/pallas_call | solution.py:549

commit v9 on v8

--- a/solution.py
+++ b/solution.py
@@ -243,10 +243,11 @@
             self.left(name)
 
 
+PIECES = 4
 N_SEND, N_RECV, N_LOCAL = 26, 54, 16
 
 
-def kernel(plan, order, panels, xa, wu, wd, za, dx, dwu, dwd, XF, GF, DF, GPB, DPB, XPB, HPB, su, sd, sw,
+def work(plan, order, panels, xa, wu, wd, za, dx, dwu, dwd, XF, GF, DF, GPB, DPB, XPB, HPB, su, sd, sw,
            wus, wds, wun, hbuf, pan, ft, rst, rrc, obuf, acc, send, recv, local):
     it, un = plan
     x, y, c = lax.axis_index("cy"), lax.axis_index("cz"), lax.axis_index("cx")
@@ -491,13 +492,20 @@
     assert tuple(cp.used.values()) == (N_SEND, N_RECV, N_LOCAL), cp.used
 
 
+def kernel(plan, order, panels, *refs):
+    pl.run_scoped(functools.partial(work, plan, order, panels, *refs), *(pltpu.SemaphoreType.DMA((n,)) for n in (N_SEND, N_RECV, N_LOCAL)))
+
+
 def write_out(dx, dwu, dwd, dx_out, dwu_out, dwd_out, sem):
-    pairs = [(a.at[i], b.at[i]) for a, b in ((dx, dx_out), (dwu, dwu_out), (dwd, dwd_out)) for i in range(a.shape[0])]
-    copies = [pltpu.make_async_copy(a, b, sem.at[i]) for i, (a, b) in enumerate(pairs)]
-    for copy in copies:
-        copy.start()
-    for copy in copies:
-        copy.wait()
+    arrays = ((dx, dx_out), (dwu, dwu_out), (dwd, dwd_out))
+    for i, (a, b) in enumerate(arrays):
+        n = a.shape[1] // PIECES
+        for j in range(a.shape[0]):
+            for p in range(PIECES):
+                rows = pl.ds(p * n, n)
+                pltpu.make_async_copy(a.at[j, rows], b.at[j, rows], sem.at[i]).start()
+    for i, (a, b) in enumerate(arrays):
+        pltpu.make_async_copy(a, b, sem.at[i]).wait()
 
 
 def solution(mesh):
@@ -533,7 +541,6 @@
             pltpu.VMEM((NB, 2, rows, dh), f32), pltpu.VMEM((NB, 2, 2, rows, dh), f32),
             pltpu.VMEM((3, CORES, sub, dh), bf),
             pltpu.VMEM((grp, sub), f32),
-            pltpu.SemaphoreType.DMA((N_SEND,)), pltpu.SemaphoreType.DMA((N_RECV,)), pltpu.SemaphoreType.DMA((N_LOCAL,)),
         ]
         any_spec = pl.BlockSpec(memory_space=pl.ANY)
         res = pl.pallas_call(
@@ -551,7 +558,7 @@
             out_shape=[jax.ShapeDtypeStruct(o.shape, bf) for o in outs],
             in_specs=[pl.BlockSpec(memory_space=pltpu.VMEM) for _ in outs],
             out_specs=[any_spec for _ in outs],
-            scratch_shapes=[pltpu.SemaphoreType.DMA((sum(o.shape[0] for o in outs),))],
+            scratch_shapes=[pltpu.SemaphoreType.DMA((len(outs),))],
             compiler_params=pltpu.CompilerParams(vmem_limit_bytes=1 << 20),
             name="write_out",
         )(*outs)

time: 352 us -> 351 us (level)
  no operation moved by 1% of the time
where the time goes in v9:
time: 351 us
  Pallas kernels  350 us (100%)
    pallas_call x1, Pallas kernels, local_step(): pl.pallas_call(functools.partial(kernel, plan, order, panels), out_shape=...  346 us

profile of v9, /device:TPU:96, one launch (start us, length us, event | category | flops | bytes accessed | tf_op | source)
XLA Modules:
  0.0 350.8 jit_solution(2710079497935795811)
XLA Ops:
  0.6 346.3 %mlp_bwd.1 = (bf16[4,128,1024]{2,1,0:T(8,128)(2,1)S(1)}, bf16[2,512,2048]{2,1,0:T(8,128)(2,1)S(1)}, bf16[2,4,512,512]{3,2,1,0:T(8,128)(2,1)S(1)}, bf16[4,4,512,1...) custom-call(bf16[4,128,1024]{2,1,0:T(8,128)(2,1)} %bitcast.9, ...), custom_call_target="tpu_custom_call" | custom-call | tf_op jit(solution)/shard_map/mlp_bwd/pallas_call | solution.py:546
  347.0 3.6 %write_out.1 = (bf16[4,128,1024]{2,1,0:T(8,128)(2,1)}, bf16[2,512,2048]{2,1,0:T(8,128)(2,1)}, bf16[2,4,512,512]{3,2,1,0:T(8,128)(2,1)}) custom-call(bf16[4,128,1024]{2,1,0:T(8,128)(2,1)S(1)} %get-tuple-element.9.dx, bf16[2,512,2048]{2,1,0:T(8,128)(2,1)S(1)} %get-tuple-element.10.dwu, bf16[2,4,512,512]{3,2,1,0:T(8,128)(2,1)S(1)} %get-tuple-element.11.dwd), custom_call_target="tpu_custom_call" | custom-call | tf_op jit(solution)/shard_map/write_out/pallas_call | solution.py:556

commit v10 on v9

--- a/solution.py
+++ b/solution.py
@@ -113,9 +113,9 @@
 
 
 ORDER = (
-    "acbdimgInhjEHGFyJosuApzteBvkflqwrxCKDML",
-    "admjbecsknfolutvzBACGIHJghipqrwxyDKELFM",
-    "yompqhsjlwunkfAgBtxCiveabzcrEDd",
+    "abicgdhjmFnIEHGJuosAyptBekvzflqwrxCKDLM",
+    "dajmbenscfkolutvzBACGIHJghipqrwxyDELKFM",
+    "gkbyAdcesvDuphBmoiwCrltjaxzqfEn",
 )
 
 
@@ -243,8 +243,8 @@
             self.left(name)
 
 
-PIECES = 4
-N_SEND, N_RECV, N_LOCAL = 26, 54, 16
+PIECES = 2
+N_SEND, N_RECV, N_LOCAL = 24, 48, 16
 
 
 def work(plan, order, panels, xa, wu, wd, za, dx, dwu, dwd, XF, GF, DF, GPB, DPB, XPB, HPB, su, sd, sw,

time: 351 us -> 351 us (level)
  no operation moved by 1% of the time
where the time goes in v10:
time: 351 us
  Pallas kernels  350 us (100%)
    pallas_call x1, Pallas kernels, local_step(): pl.pallas_call(functools.partial(kernel, plan, order, panels), out_shape=...  346 us

profile of v10, /device:TPU:96, one launch (start us, length us, event | category | flops | bytes accessed | tf_op | source)
XLA Modules:
  0.0 350.8 jit_solution(11256157361559294732)
XLA Ops:
  0.6 346.4 %mlp_bwd.1 = (bf16[4,128,1024]{2,1,0:T(8,128)(2,1)S(1)}, bf16[2,512,2048]{2,1,0:T(8,128)(2,1)S(1)}, bf16[2,4,512,512]{3,2,1,0:T(8,128)(2,1)S(1)}, bf16[4,4,512,1...) custom-call(bf16[4,128,1024]{2,1,0:T(8,128)(2,1)} %bitcast.9, ...), custom_call_target="tpu_custom_call" | custom-call | tf_op jit(solution)/shard_map/mlp_bwd/pallas_call | solution.py:546
  347.0 3.6 %write_out.1 = (bf16[4,128,1024]{2,1,0:T(8,128)(2,1)}, bf16[2,512,2048]{2,1,0:T(8,128)(2,1)}, bf16[2,4,512,512]{3,2,1,0:T(8,128)(2,1)}) custom-call(bf16[4,128,1024]{2,1,0:T(8,128)(2,1)S(1)} %get-tuple-element.9.dx, bf16[2,512,2048]{2,1,0:T(8,128)(2,1)S(1)} %get-tuple-element.10.dwu, bf16[2,4,512,512]{3,2,1,0:T(8,128)(2,1)S(1)} %get-tuple-element.11.dwd), custom_call_target="tpu_custom_call" | custom-call | tf_op jit(solution)/shard_map/write_out/pallas_call | solution.py:556

commit v11 on v9

--- a/solution.py
+++ b/solution.py
@@ -21,6 +21,7 @@
 GROUPS = ((0, 0, 8), (1, 0, 8), (2, 0, 8), (3, 0, 4), (3, 4, 4))
 NB = 4
 NG = len(GROUPS)
+LAST = NG - 1
 EARLY = 2
 X, G = 0, 1
 
@@ -287,7 +288,16 @@
         _, first, n = group(r)
         return pl.ds(RING * first, RING * n)
 
-    def copies_of(name):
+    def of_part(copies, part, turned=False):
+        return [c for i, c in enumerate(copies) if part is None or (i == part) != turned]
+
+    def in_halves(r, kinds, body):
+        for t in range(CORES):
+            body(t)
+            for kind in kinds:
+                cp.add((kind, r), copies_of((kind, r), t))
+
+    def copies_of(name, part=None):
         kind, a, r = name[0], name[-2:][0], name[-1]
         both = lambda right, left: [right + ("R",), left + ("L",)]
         updn = lambda up, down: [up + ("U",), down + ("N",)]
@@ -339,8 +349,9 @@
             return [(obuf.at[2, :, span(r)], DF.at[0, b, :, span(r)], None)]
         if kind == CS:
             b = group(r)[0]
-            m = DF.at[0, b, :, span(r)] if staged(r) else obuf.at[2, :, span(r)]
-            return both((m, DF.at[3, b, :, span(r)]), (m, DF.at[1, b, :, span(r)]))
+            h = pl.ds(0, CORES) if part is None else part
+            m = DF.at[0, b, h, span(r)] if staged(r) else obuf.at[2, h, span(r)]
+            return both((m, DF.at[3, b, h, span(r)]), (m, DF.at[1, b, h, span(r)]))
         if kind == CR:
             b, first, n = group(r)
             f, s = (pl.ds(RING * first + h * 2 * n, 2 * n) for h in range(2))
@@ -351,9 +362,9 @@
             own = lambda k: pl.ds(k * n, n)
             rs = pl.ds(first, n)
             if kind == Q2:
-                return updn((f.at[0, own(2)], rst.at[b, 0, rs]), (f.at[1, own(2)], rst.at[b, 1, rs]))
+                return of_part(updn((f.at[0, own(2)], rst.at[b, 0, rs]), (f.at[1, own(2)], rst.at[b, 1, rs])), part)
             if kind == QD:
-                return updn((f.at[1, own(1)], rrc.at[b, 0, 1, rs]), (f.at[0, own(3)], rrc.at[b, 1, 0, rs]))
+                return of_part(updn((f.at[1, own(1)], rrc.at[b, 0, 1, rs]), (f.at[0, own(3)], rrc.at[b, 1, 0, rs])), part, True)
             return updn((f.at[0, own(1)], rrc.at[b, 0, 0, rs]), (f.at[1, own(3)], rrc.at[b, 1, 1, rs]))
         if kind in (L1, L2, L3):
             b, _, n = group(r)
@@ -384,7 +395,10 @@
             out = d if out is None else out + d
         return out
 
-    def loop(n, body):
+    def at_tile(t):
+        return pl.ds(t * sub if isinstance(t, int) else pl.multiple_of(t * sub, sub), sub)
+
+    def loop(body, n=CORES):
         def step(i, carry):
             body(i)
             return carry
@@ -402,7 +416,7 @@
                 ns = pl.ds(pl.multiple_of(t * sub, sub), sub)
                 s = total([(p[j, rows, h * dh:(h + 1) * dh], wus[2 * j + h, :, ns], NN) for j in range(RING) for h in range(2)])
                 hbuf[b, span(r), ns] = s.astype(jnp.bfloat16)
-            loop(2, body)
+            loop(body)
         elif kind == M2:
             p = pan.at[slot_of[L2, r]]
             if r > 0 and staged(r - 1):
@@ -410,7 +424,7 @@
             step = min(32, RING * n)
 
             def body(t):
-                ns = pl.ds(pl.multiple_of(t * sub, sub), sub)
+                ns = at_tile(t)
                 acc[rows, :] = total([(p[j, rows, :], wds[2 * j + t], NT) for j in range(RING)])
 
                 def elem(e):
@@ -419,8 +433,11 @@
                     g, s = gelu_parts(hbuf[b, hs, ns].astype(jnp.float32))
                     hbuf[b, hs, ns] = g.astype(jnp.bfloat16)
                     obuf[2, t, hs, :] = (acc[rs, :] * s).astype(jnp.bfloat16)
-                loop(RING * n // step, elem)
-            loop(2, body)
+                loop(elem, RING * n // step)
+            if r == LAST:
+                in_halves(r, [CS], body)
+            else:
+                loop(body)
         elif kind == M3:
             p = pan.at[slot_of[L3, r]]
             if r >= 2:
@@ -430,7 +447,10 @@
 
             def body(t):
                 f[t, rows, :] = total([(p[j, rows, :], wun[2 * j + t], NT) for j in range(RING)])
-            loop(2, body)
+            if r == LAST:
+                in_halves(r, [Q2, QD], body)
+            else:
+                loop(body)
         elif kind in (M5, M4):
             i0, m = PARTS[r]
             s0, s1 = (slot_of[L5 if kind == M5 else L4, i] for i in (i0, i0 + m - 1))
@@ -452,7 +472,7 @@
                     obuf[i0 + e, t] = s.astype(jnp.bfloat16)
                 else:
                     dwu[t, :, cols(j0 + e * (j1 - j0))] = s.astype(jnp.bfloat16)
-            loop(2 * m, body)
+            loop(body, CORES * m)
         else:
             b, first, n = group(r)
             f = ft.at[r % 2]
@@ -485,7 +505,8 @@
             for w in {LX: (0,), LH: (1,)}.get(name[0], ()):
                 for p in range(3):
                     cp.left((WP, w, p))
-            cp.add(name, copies_of(name))
+            if name not in cp.by_name:
+                cp.add(name, copies_of(name))
         else:
             unit(name)
     cp.finish()

time: 351 us -> 351 us (level)
  no operation moved by 1% of the time
where the time goes in v11:
time: 351 us
  Pallas kernels  350 us (100%)
    pallas_call x1, Pallas kernels, local_step(): pl.pallas_call(functools.partial(kernel, plan, order, panels), out_shape=...  346 us

profile of v11, /device:TPU:96, one launch (start us, length us, event | category | flops | bytes accessed | tf_op | source)
XLA Modules:
  0.0 350.8 jit_solution(5068565838844129683)
XLA Ops:
  0.6 346.4 %mlp_bwd.1 = (bf16[4,128,1024]{2,1,0:T(8,128)(2,1)S(1)}, bf16[2,512,2048]{2,1,0:T(8,128)(2,1)S(1)}, bf16[2,4,512,512]{3,2,1,0:T(8,128)(2,1)S(1)}, bf16[4,4,512,1...) custom-call(bf16[4,128,1024]{2,1,0:T(8,128)(2,1)} %bitcast.9, ...), custom_call_target="tpu_custom_call" | custom-call | tf_op jit(solution)/shard_map/mlp_bwd/pallas_call | solution.py:567
  347.0 3.6 %write_out.1 = (bf16[4,128,1024]{2,1,0:T(8,128)(2,1)}, bf16[2,512,2048]{2,1,0:T(8,128)(2,1)}, bf16[2,4,512,512]{3,2,1,0:T(8,128)(2,1)}) custom-call(bf16[4,128,1024]{2,1,0:T(8,128)(2,1)S(1)} %get-tuple-element.9.dx, bf16[2,512,2048]{2,1,0:T(8,128)(2,1)S(1)} %get-tuple-element.10.dwu, bf16[2,4,512,512]{3,2,1,0:T(8,128)(2,1)S(1)} %get-tuple-element.11.dwd), custom_call_target="tpu_custom_call" | custom-call | tf_op jit(solution)/shard_map/write_out/pallas_call | solution.py:577

commit v12 on v9

--- a/solution.py
+++ b/solution.py
@@ -248,7 +248,7 @@
 
 
 def work(plan, order, panels, xa, wu, wd, za, dx, dwu, dwd, XF, GF, DF, GPB, DPB, XPB, HPB, su, sd, sw,
-           wus, wds, wun, hbuf, pan, ft, rst, rrc, obuf, acc, send, recv, local):
+           wus, wds, wun, hbuf, pan, ft, rst, rrc, obuf, acc, send, recv, local, ready):
     it, un = plan
     x, y, c = lax.axis_index("cy"), lax.axis_index("cz"), lax.axis_index("cx")
     peers = {
@@ -257,9 +257,17 @@
         "P": ("cx", 1 - c),
     }
     barrier = pltpu.get_barrier_semaphore()
-    for axis, idx in peers.values():
-        pl.semaphore_signal(barrier, inc=1, device_id={axis: idx}, device_id_type=MESH)
-    pl.semaphore_wait(barrier, len(peers))
+    def tell(semaphore, to):
+        axis, idx = peers[to]
+        pl.semaphore_signal(semaphore, device_id={axis: idx}, device_id_type=MESH)
+
+    ring = [to for to in peers if to != "P"]
+    for to in ring:
+        tell(barrier, to)
+    pl.when(c == 0)(lambda: tell(barrier, "P"))
+    pl.semaphore_wait(barrier, len(ring) + c)
+    pl.when(c != 0)(lambda: tell(ready, "P"))
+    waited = []
 
     cp = Copies(send, recv, local, peers)
     blk_rows = xa.shape[1]
@@ -485,7 +493,11 @@
             for w in {LX: (0,), LH: (1,)}.get(name[0], ()):
                 for p in range(3):
                     cp.left((WP, w, p))
-            cp.add(name, copies_of(name))
+            copies = copies_of(name)
+            if not waited and any(to == "P" for _, _, to in copies):
+                waited.append(name)
+                pl.when(c == 0)(lambda: pl.semaphore_wait(ready))
+            cp.add(name, copies)
         else:
             unit(name)
     cp.finish()
@@ -493,7 +505,7 @@
 
 
 def kernel(plan, order, panels, *refs):
-    pl.run_scoped(functools.partial(work, plan, order, panels, *refs), *(pltpu.SemaphoreType.DMA((n,)) for n in (N_SEND, N_RECV, N_LOCAL)))
+    pl.run_scoped(functools.partial(work, plan, order, panels, *refs), *(pltpu.SemaphoreType.DMA((n,)) for n in (N_SEND, N_RECV, N_LOCAL)), pltpu.SemaphoreType.REGULAR)
 
 
 def write_out(dx, dwu, dwd, dx_out, dwu_out, dwd_out, sem):

time: 351 us -> 351 us (level)
  no operation moved by 1% of the time
where the time goes in v12:
time: 351 us
  Pallas kernels  350 us (100%)
    pallas_call x1, Pallas kernels, local_step(): pl.pallas_call(functools.partial(kernel, plan, order, panels), out_shape=...  346 us

profile of v12, /device:TPU:96, one launch (start us, length us, event | category | flops | bytes accessed | tf_op | source)
XLA Modules:
  0.0 350.8 jit_solution(5808430707998108620)
XLA Ops:
  0.6 346.3 %mlp_bwd.1 = (bf16[4,128,1024]{2,1,0:T(8,128)(2,1)S(1)}, bf16[2,512,2048]{2,1,0:T(8,128)(2,1)S(1)}, bf16[2,4,512,512]{3,2,1,0:T(8,128)(2,1)S(1)}, bf16[4,4,512,1...) custom-call(bf16[4,128,1024]{2,1,0:T(8,128)(2,1)} %bitcast.9, ...), custom_call_target="tpu_custom_call" | custom-call | tf_op jit(solution)/shard_map/mlp_bwd/pallas_call | solution.py:558
  347.0 3.6 %write_out.1 = (bf16[4,128,1024]{2,1,0:T(8,128)(2,1)}, bf16[2,512,2048]{2,1,0:T(8,128)(2,1)}, bf16[2,4,512,512]{3,2,1,0:T(8,128)(2,1)}) custom-call(bf16[4,128,1024]{2,1,0:T(8,128)(2,1)S(1)} %get-tuple-element.9.dx, bf16[2,512,2048]{2,1,0:T(8,128)(2,1)S(1)} %get-tuple-element.10.dwu, bf16[2,4,512,512]{3,2,1,0:T(8,128)(2,1)S(1)} %get-tuple-element.11.dwd), custom_call_target="tpu_custom_call" | custom-call | tf_op jit(solution)/shard_map/write_out/pallas_call | solution.py:568

commit v13 on v11

--- a/solution.py
+++ b/solution.py
@@ -114,9 +114,9 @@
 
 
 ORDER = (
-    "acbdimgInhjEHGFyJosuApzteBvkflqwrxCKDML",
-    "admjbecsknfolutvzBACGIHJghipqrwxyDKELFM",
-    "yompqhsjlwunkfAgBtxCiveabzcrEDd",
+    "abicgdhjmFnIEHGJuosAyptBekvzflqwrxCKDLM",
+    "dajmbenscfkolutvzBACGIHJghipqrwxyDELKFM",
+    "gkbyAdcesvDuphBmoiwCrltjaxzqfEn",
 )
 
 
@@ -245,11 +245,11 @@
 
 
 PIECES = 4
-N_SEND, N_RECV, N_LOCAL = 26, 54, 16
+N_SEND, N_RECV, N_LOCAL = 24, 48, 16
 
 
 def work(plan, order, panels, xa, wu, wd, za, dx, dwu, dwd, XF, GF, DF, GPB, DPB, XPB, HPB, su, sd, sw,
-           wus, wds, wun, hbuf, pan, ft, rst, rrc, obuf, acc, send, recv, local):
+           wus, wds, wun, hbuf, pan, ft, rst, rrc, obuf, acc, send, recv, local, ready):
     it, un = plan
     x, y, c = lax.axis_index("cy"), lax.axis_index("cz"), lax.axis_index("cx")
     peers = {
@@ -258,9 +258,17 @@
         "P": ("cx", 1 - c),
     }
     barrier = pltpu.get_barrier_semaphore()
-    for axis, idx in peers.values():
-        pl.semaphore_signal(barrier, inc=1, device_id={axis: idx}, device_id_type=MESH)
-    pl.semaphore_wait(barrier, len(peers))
+    def tell(semaphore, to):
+        axis, idx = peers[to]
+        pl.semaphore_signal(semaphore, device_id={axis: idx}, device_id_type=MESH)
+
+    ring = [to for to in peers if to != "P"]
+    for to in ring:
+        tell(barrier, to)
+    pl.when(c == 0)(lambda: tell(barrier, "P"))
+    pl.semaphore_wait(barrier, len(ring) + c)
+    pl.when(c != 0)(lambda: tell(ready, "P"))
+    waited = []
 
     cp = Copies(send, recv, local, peers)
     blk_rows = xa.shape[1]
@@ -505,8 +513,13 @@
             for w in {LX: (0,), LH: (1,)}.get(name[0], ()):
                 for p in range(3):
                     cp.left((WP, w, p))
-            if name not in cp.by_name:
-                cp.add(name, copies_of(name))
+            if name in cp.by_name:
+                continue
+            copies = copies_of(name)
+            if not waited and any(to == "P" for _, _, to in copies):
+                waited.append(name)
+                pl.when(c == 0)(lambda: pl.semaphore_wait(ready))
+            cp.add(name, copies)
         else:
             unit(name)
     cp.finish()
@@ -514,7 +527,7 @@
 
 
 def kernel(plan, order, panels, *refs):
-    pl.run_scoped(functools.partial(work, plan, order, panels, *refs), *(pltpu.SemaphoreType.DMA((n,)) for n in (N_SEND, N_RECV, N_LOCAL)))
+    pl.run_scoped(functools.partial(work, plan, order, panels, *refs), *(pltpu.SemaphoreType.DMA((n,)) for n in (N_SEND, N_RECV, N_LOCAL)), pltpu.SemaphoreType.REGULAR)
 
 
 def write_out(dx, dwu, dwd, dx_out, dwu_out, dwd_out, sem):

time: 351 us -> 351 us (level)
  no operation moved by 1% of the time
where the time goes in v13:
time: 351 us
  Pallas kernels  350 us (100%)
    pallas_call x1, Pallas kernels, local_step(): pl.pallas_call(functools.partial(kernel, plan, order, panels), out_shape=...  346 us

profile of v13, /device:TPU:96, one launch (start us, length us, event | category | flops | bytes accessed | tf_op | source)
XLA Modules:
  0.0 350.8 jit_solution(10928458612136579969)
XLA Ops:
  0.6 346.4 %mlp_bwd.1 = (bf16[4,128,1024]{2,1,0:T(8,128)(2,1)S(1)}, bf16[2,512,2048]{2,1,0:T(8,128)(2,1)S(1)}, bf16[2,4,512,512]{3,2,1,0:T(8,128)(2,1)S(1)}, bf16[4,4,512,1...) custom-call(bf16[4,128,1024]{2,1,0:T(8,128)(2,1)} %bitcast.9, ...), custom_call_target="tpu_custom_call" | custom-call | tf_op jit(solution)/shard_map/mlp_bwd/pallas_call | solution.py:580
  347.0 3.6 %write_out.1 = (bf16[4,128,1024]{2,1,0:T(8,128)(2,1)}, bf16[2,512,2048]{2,1,0:T(8,128)(2,1)}, bf16[2,4,512,512]{3,2,1,0:T(8,128)(2,1)}) custom-call(bf16[4,128,1024]{2,1,0:T(8,128)(2,1)S(1)} %get-tuple-element.9.dx, bf16[2,512,2048]{2,1,0:T(8,128)(2,1)S(1)} %get-tuple-element.10.dwu, bf16[2,4,512,512]{3,2,1,0:T(8,128)(2,1)S(1)} %get-tuple-element.11.dwd), custom_call_target="tpu_custom_call" | custom-call | tf_op jit(solution)/shard_map/write_out/pallas_call | solution.py:590

commit v14 on v9

--- a/solution.py
+++ b/solution.py
@@ -1,6 +1,7 @@
 import functools
 import math
 import string
+import itertools
 
 import jax
 import jax.numpy as jnp
@@ -243,7 +244,7 @@
             self.left(name)
 
 
-PIECES = 4
+PIECES = 8
 N_SEND, N_RECV, N_LOCAL = 26, 54, 16
 
 
@@ -497,13 +498,15 @@
 
 
 def write_out(dx, dwu, dwd, dx_out, dwu_out, dwd_out, sem):
-    arrays = ((dx, dx_out), (dwu, dwu_out), (dwd, dwd_out))
+    arrays = ((dwd, dwd_out), (dwu, dwu_out), (dx, dx_out))
     for i, (a, b) in enumerate(arrays):
-        n = a.shape[1] // PIECES
-        for j in range(a.shape[0]):
-            for p in range(PIECES):
-                rows = pl.ds(p * n, n)
-                pltpu.make_async_copy(a.at[j, rows], b.at[j, rows], sem.at[i]).start()
+        lead = a.shape[:-2]
+        pieces = PIECES if a is dwu else PIECES // 4
+        n = a.shape[-2] // pieces
+        for place in itertools.product(*map(range, lead)):
+            for p in range(pieces):
+                part = place + (pl.ds(p * n, n),)
+                pltpu.make_async_copy(a.at[part], b.at[part], sem.at[i]).start()
     for i, (a, b) in enumerate(arrays):
         pltpu.make_async_copy(a, b, sem.at[i]).wait()
 

time: 351 us -> 351 us (level)
  no operation moved by 1% of the time
where the time goes in v14:
time: 351 us
  Pallas kernels  350 us (100%)
    pallas_call x1, Pallas kernels, local_step(): pl.pallas_call(functools.partial(kernel, plan, order, panels), out_shape=...  346 us

profile of v14, /device:TPU:96, one launch (start us, length us, event | category | flops | bytes accessed | tf_op | source)
XLA Modules:
  0.0 350.7 jit_solution(5500548347544079042)
XLA Ops:
  0.6 346.3 %mlp_bwd.1 = (bf16[4,128,1024]{2,1,0:T(8,128)(2,1)S(1)}, bf16[2,512,2048]{2,1,0:T(8,128)(2,1)S(1)}, bf16[2,4,512,512]{3,2,1,0:T(8,128)(2,1)S(1)}, bf16[4,4,512,1...) custom-call(bf16[4,128,1024]{2,1,0:T(8,128)(2,1)} %bitcast.9, ...), custom_call_target="tpu_custom_call" | custom-call | tf_op jit(solution)/shard_map/mlp_bwd/pallas_call | solution.py:549
  347.0 3.6 %write_out.1 = (bf16[4,128,1024]{2,1,0:T(8,128)(2,1)}, bf16[2,512,2048]{2,1,0:T(8,128)(2,1)}, bf16[2,4,512,512]{3,2,1,0:T(8,128)(2,1)}) custom-call(bf16[4,128,1024]{2,1,0:T(8,128)(2,1)S(1)} %get-tuple-element.9.dx, bf16[2,512,2048]{2,1,0:T(8,128)(2,1)S(1)} %get-tuple-element.10.dwu, bf16[2,4,512,512]{3,2,1,0:T(8,128)(2,1)S(1)} %get-tuple-element.11.dwd), custom_call_target="tpu_custom_call" | custom-call | tf_op jit(solution)/shard_map/write_out/pallas_call | solution.py:559
